TPU v7x, 256 devices: a whole 4x4x8 slice. The times are simulated.
256 devices in a mesh: dp: 64 (over y, z_hi, x), tensor: 4 (over z_lo, core).
Axes of the slice: x: 4, y: 4, z: 8 (z_hi: 4, z_lo: 2; z = z_hi * 2 + z_lo), core: 2. Of those that a mesh axis runs over, the one named last changes fastest.
Arguments:
- activations: bfloat16 [32768, 4096], P('dp'), may hold values from -1000 to 1000
- norm_gain: bfloat16 [4096], replicated, may hold values from 0.5 to 1.5
- query_blocks: bfloat16 [128, 32, 4096], P('dp', None, 'tensor'), may hold values from -64 to 64
- query_scales: int32 [128, 1, 4096], P('dp', None, 'tensor'), may hold values from -9 to -5
- key_blocks: bfloat16 [128, 32, 512], P('dp', None, 'tensor'), may hold values from -64 to 64
- key_scales: int32 [128, 1, 512], P('dp', None, 'tensor'), may hold values from -9 to -5
- value_blocks: bfloat16 [128, 32, 512], P('dp', None, 'tensor'), may hold values from -6 to 6
- value_scales: int32 [128, 1, 512], P('dp', None, 'tensor'), may hold values from -9 to -5
- output_blocks: bfloat16 [128, 32, 4096], P('tensor', None, 'dp'), may hold values from -6 to 6
- output_scales: int32 [128, 1, 4096], P('tensor', None, 'dp'), may hold values from -9 to -5
Outputs:
- attended: bfloat16 [32768, 4096], P('dp')
All inputs are finite; a program needn't handle non-finite values.
Results may differ from a plain program's by a relative error of at most 0.015.
The roundings to bfloat16 on the way count: a program that leaves them out, or rounds other values in their place, can miss the bound.
Values may be sent and summed in bfloat16 or wider, within the bound.
A program may use at most 128 MiB of HBM per device.

v0:
```python
import math

import jax
import jax.numpy as jnp
from jax import lax
from jax.sharding import PartitionSpec as P

HEAD_DIM = 128
SEQ = 256


EPS = 1e-05
ROPE_BASE = 500000.0


def turned_gather(arrays, axis, dims):
    turned = [jnp.moveaxis(a, dim, 0) for a, dim in zip(arrays, dims)]
    widths = [t[0].size for t in turned]
    both = jnp.concatenate([t.reshape(-1, w) for t, w in zip(turned, widths)], axis=1)
    out = lax.all_gather(both, axis, axis=0, tiled=True)
    blocks = jnp.split(out, [sum(widths[:k]) for k in range(1, len(widths))], axis=1)
    return tuple(
        (
            jnp.moveaxis(b.reshape(-1, *t.shape[1:]), 0, dim)
            for b, t, dim in zip(blocks, turned, dims)
        )
    )


def side_by_side(arrays, axis, dim, along):
    widths = [math.prod(a.shape[along:]) for a in arrays]
    both = jnp.concatenate(
        [a.reshape(*a.shape[:along], w) for a, w in zip(arrays, widths)], axis=along
    )
    out = lax.all_gather(both, axis, axis=dim, tiled=True)
    blocks = jnp.split(out, [sum(widths[:k]) for k in range(1, len(widths))], axis=along)
    return tuple((b.reshape(*out.shape[:along], *a.shape[along:]) for a, b in zip(arrays, blocks)))


def dequant(blocks, scales):
    factor = jnp.exp2(scales.astype(jnp.float32)).astype(blocks.dtype)
    weight = blocks * factor
    return weight.reshape(weight.shape[0] * weight.shape[1], weight.shape[2])


def rotate_pairs(states, positions):
    half_dim = states.shape[-1] // 2
    frequency = jnp.exp(
        -math.log(ROPE_BASE) * jnp.arange(half_dim, dtype=jnp.float32) * 2.0 / states.shape[-1]
    )
    angles = positions.astype(jnp.float32)[:, None] * frequency[None, :]
    cosine = jnp.cos(angles)[None, :, None, :]
    sine_part = jnp.sin(angles)[None, :, None, :]
    first = states[..., :half_dim]
    second = states[..., half_dim:]
    return jnp.concatenate(
        [first * cosine - second * sine_part, second * cosine + first * sine_part], axis=-1
    )


def attend(query_states, key_states, value_states, kv_count):
    tokens_here = query_states.shape[0]
    count = tokens_here // SEQ
    positions = jnp.arange(SEQ, dtype=jnp.int32)
    queries = rotate_pairs(query_states.reshape(count, SEQ, -1, HEAD_DIM), positions).astype(
        jnp.bfloat16
    )
    rotated_keys = rotate_pairs(
        key_states.reshape(count, SEQ, kv_count, HEAD_DIM), positions
    ).astype(jnp.bfloat16)
    value_heads = value_states.astype(jnp.bfloat16).reshape(count, SEQ, kv_count, HEAD_DIM)
    group_size = queries.shape[2] // kv_count
    queries = queries.reshape(count, SEQ, kv_count, group_size, HEAD_DIM)
    scores = jnp.einsum(
        "sqkgd,stkd->skgqt", queries, rotated_keys, preferred_element_type=jnp.float32
    ) * HEAD_DIM ** (-0.5)
    visible = positions[:, None] >= positions[None, :]
    scores = jnp.where(visible, scores, -jnp.inf)
    attn_weights = jax.nn.softmax(scores, axis=-1).astype(jnp.bfloat16)
    context = jnp.einsum(
        "skgqt,stkd->sqkgd", attn_weights, value_heads, preferred_element_type=jnp.float32
    )
    return context.astype(jnp.bfloat16).reshape(tokens_here, -1)


def shards(
    activations,
    norm_gain,
    query_blocks,
    query_scales,
    key_blocks,
    key_scales,
    value_blocks,
    value_scales,
    output_blocks,
    output_scales,
):
    query_exps = query_scales.astype(jnp.bfloat16)
    key_exps = key_scales.astype(jnp.bfloat16)
    value_exps = value_scales.astype(jnp.bfloat16)
    output_exps = output_scales.astype(jnp.bfloat16)
    output_whole = turned_gather((output_blocks, output_exps), "dp", (2, 2))
    wide_rows = activations.astype(jnp.float32)
    inverse = lax.rsqrt(jnp.mean(wide_rows * wide_rows, axis=-1, keepdims=True) + EPS)
    normed = (wide_rows * inverse * norm_gain.astype(jnp.float32)).astype(jnp.bfloat16)

    def product(blocks, scales):
        return jnp.dot(normed, dequant(blocks, scales), preferred_element_type=jnp.float32)

    pieces = side_by_side(
        (query_blocks, query_exps, key_blocks, key_exps, value_blocks, value_exps), "dp", 0, 1
    )
    query_states = product(pieces[0], pieces[1])
    key_states = product(pieces[2], pieces[3])
    value_states = product(pieces[4], pieces[5])
    context = attend(query_states, key_states, value_states, key_blocks.shape[2] // HEAD_DIM)
    partial_value = jnp.dot(
        context, dequant(output_whole[0], output_whole[1]), preferred_element_type=jnp.float32
    )
    return lax.psum(partial_value.astype(jnp.bfloat16), "tensor")


def solution(mesh):
    placed = (
        P("dp", None),
        P(),
        P("dp", None, "tensor"),
        P("dp", None, "tensor"),
        P("dp", None, "tensor"),
        P("dp", None, "tensor"),
        P("dp", None, "tensor"),
        P("dp", None, "tensor"),
        P("tensor", None, "dp"),
        P("tensor", None, "dp"),
    )
    return jax.shard_map(
        shards, mesh=mesh, in_specs=placed, out_specs=P("dp", None), check_vma=False
    )
```

profile of v0, /device:TPU:1, one launch (start us, length us, event | category | flops | bytes accessed | tf_op | source)
XLA Modules:
  0.0 459.1 jit_solution(9904622550752400796)
XLA Ops:
  6.5 0.0 all-gather.4.cloned.1.call-start
  6.5 0.7 convert_bitcast_fusion
  7.3 1.0 pad_maximum_fusion
  8.3 0.8 copy.48
  9.1 0.0 all-gather.4.cloned.1.call-update
  9.1 0.0 all-gather.6.cloned.1.call-start
  9.2 1.0 copy.64
  10.2 0.1 constant_dynamic-update-slice_fusion.3
  10.3 0.7 constant_dynamic-update-slice_fusion.2
  11.0 0.7 bitcast_dynamic-update-slice_fusion.1
  11.8 0.7 constant_dynamic-update-slice_fusion.1
  12.4 0.7 bitcast_dynamic-update-slice_fusion
  13.2 0.7 constant_dynamic-update-slice_fusion
  13.9 0.0 copy-start.2
  13.9 0.7 copy-done.2
  14.6 0.0 all-gather.6.cloned.1.call-update
  14.6 0.0 all-reduce.2.cloned.1.call-start
  14.6 0.0 copy-start
  14.6 0.9 convert_element_type.104
  15.5 3.3 fusion
  18.9 0.3 multiply_cosine_fusion
  19.2 0.0 copy-done
  19.2 3.6 fusion.2
  22.8 106.9 %all-gather.4.cloned.1.call-done = bf16[4096,1056]{1,0:T(8,128)(2,1)} async-done(((bf16[64,1056]{1,0:T(8,128)(2,1)}), bf16[4096,1056]{1,0:T(8,128)(2,1)}) %all-gather.4.cloned.1.call-update) | async-done | bytes 8650768 | tf_op jit(solution)/shard_map/all_gather | solution.py:20
  129.7 1.6 fusion.14
  131.3 0.3 copy.50
  131.6 7.7 %split.38 = bf16[4096,1024]{1,0:T(8,128)(2,1)} slice(bf16[4096,1056]{1,0:T(8,128)(2,1)} %all-gather.4.cloned.1.call-done), slice={[0:4096], [0:1024]} | slice | bytes 16777216 | tf_op jit(solution)/shard_map/split | solution.py:21
  139.3 11.4 %copy.63 = bf16[4096,1024]{0,1:T(8,128)(2,1)} copy(bf16[4096,1024]{1,0:T(8,128)(2,1)} %split.38) | data formatting | bytes 16777216
  150.7 7.4 %broadcast_multiply_fusion = bf16[32,32,4096]{2,1,0:T(8,128)(2,1)} fusion(bf16[32,32,4096]{2,1,0:T(8,128)(2,1)} %bitcast.115, bf16[32,4096]{1,0:T(8,128)(2,1)S(1)} %copy.50), kind=kLoop, calls=%fused_computation.8 | loop fusion | flops 4194304 | bytes 17039360 | tf_op jit(solution)/shard_map/mul | solution.py:42
  158.1 97.6 %all-gather.6.cloned.1.call-done = bf16[64,2,42240]{2,1,0:T(2,128)(2,1)} async-done(((bf16[1,2,42240]{2,1,0:T(2,128)(2,1)}), bf16[64,2,42240]{2,1,0:T(2,128)(2,1)}) %all-gather.6.cloned.1.call-update) | async-done | bytes 10813456 | tf_op jit(solution)/shard_map/all_gather | solution.py:35
  255.7 14.6 %reshape.197 = bf16[128,42240]{1,0:T(8,128)(2,1)} reshape(bf16[64,2,42240]{2,1,0:T(2,128)(2,1)} %all-gather.6.cloned.1.call-done) | data formatting | bytes 21626880
  270.4 0.8 exponential_convert_fusion.2
  271.2 1.0 exponential_convert_fusion.1
  272.2 7.3 %split.36 = bf16[128,32768]{1,0:T(8,128)(2,1)} slice(bf16[128,42240]{1,0:T(8,128)(2,1)} %reshape.197), slice={[0:128], [0:32768]} | slice | bytes 16777216 | tf_op jit(solution)/shard_map/split | solution.py:36
  279.5 0.1 mul.220
  279.7 1.9 bitcast_multiply_fusion.1
  281.6 13.5 %reshape.189 = bf16[4096,1024]{1,0:T(8,128)(2,1)} reshape(bf16[128,32768]{1,0:T(8,128)(2,1)} %split.36) | data formatting | bytes 16777216 | tf_op jit(solution)/shard_map/reshape | solution.py:37
  295.1 7.2 %bitcast_multiply_fusion = bf16[4096,1024]{1,0:T(8,128)(2,1)} fusion(bf16[4096,1024]{1,0:T(8,128)(2,1)} %reshape.189, bf16[128,1024]{1,0:T(8,128)(2,1)S(1)} %exponential_convert_fusion.1), kind=kLoop, calls=%fused_computation.5 | loop fusion | flops 4194304 | bytes 17039360 | tf_op jit(solution)/shard_map/mul | solution.py:42
  302.3 11.4 %copy.62 = bf16[1024,4096]{1,0:T(8,128)(2,1)} copy(bf16[1024,4096]{0,1:T(8,128)(2,1)} %bitcast.116) | data formatting | bytes 16777216 | tf_op jit(solution)/shard_map/dot_general | solution.py:108
  313.7 0.5 mul.223
  314.3 0.5 reshape.187
  314.8 0.0 copy-start.1
  314.8 0.1 bitcast_multiply_fusion.2
  314.9 3.6 convolution_convert_fusion.1
  318.5 0.0 copy-done.1
  318.5 7.4 %fusion.30 = f32[2,256,8,128]{1,3,2,0:T(8,128)S(1)} fusion(bf16[2,256,4096,1]{2,1,3,0:T(8,128)(2,1)S(1)} %bitcast.117, bf16[8,128,4096,1]{2,1,0,3:T(8,128)(2,1)} %bitcast.120), kind=kOutput, calls=%fused_computation.62 | convolution fusion | flops 4294967296 | bytes 14680064 | tf_op jit(solution)/shard_map/dot_general | solution.py:108
  325.9 1.5 convolution_bitcast_fusion
  327.4 0.3 subtract_convert_fusion
  327.8 0.8 fusion.4
  328.6 0.9 fusion.3
  329.5 1.3 fusion.11
  330.8 0.8 copy.46
  331.6 9.4 %convolution_convert_fusion = bf16[512,4096]{1,0:T(8,128)(2,1)} fusion(bf16[1024,4096]{1,0:T(8,128)(2,1)} %bitcast.119, bf16[64,8,8,128]{3,2,1,0:T(8,128)(2,1)S(1)} %bitcast.122), kind=kOutput, calls=%fused_computation.6 | convolution fusion | flops 4297064448 | bytes 13631488 | tf_op jit(solution)/shard_map/dot_general | solution.py:117
  341.0 0.0 all-reduce.2.cloned.1.call-update
  341.0 106.9 %all-reduce.2.cloned.1.call-done = bf16[512,4096]{1,0:T(8,128)(2,1)} async-done(((bf16[512,4096]{1,0:T(8,128)(2,1)}), bf16[512,4096]{1,0:T(8,128)(2,1)}) %all-reduce.2.cloned.1.call-update) | async-done | bytes 4194320 | tf_op jit(solution)/shard_map/psum | solution.py:120
  447.9 4.7 %copy.87 = bf16[512,4096]{1,0:T(8,128)(2,1)} copy(bf16[512,4096]{1,0:T(8,128)(2,1)} %all-reduce.2.cloned.1.call-done) | data formatting | bytes 8388608
  (5 shorter events, 0.1 us)
Async XLA Ops:
  6.5 123.2 %all-gather.4.cloned.1.call-start = ((), (), s32[]{:S(2)}) async-start(), calls=%async_computation | async-start | bytes 9584640 | tf_op jit(solution)/shard_map/all_gather | solution.py:20
  9.1 246.6 %all-gather.6.cloned.1.call-start = ((), (), s32[]{:S(2)}) async-start(), calls=%async_computation.2 | async-start | bytes 10982400 | tf_op jit(solution)/shard_map/all_gather | solution.py:35
  13.9 0.7 copy-start.2
  14.6 433.3 %all-reduce.2.cloned.1.call-start = ((), (), s32[]{:S(2)}) async-start(), calls=%async_computation.1 | async-start | bytes 8388608 | tf_op jit(solution)/shard_map/psum | solution.py:120
  14.6 4.5 copy-start
  314.8 3.7 copy-start.1
Sparse Core Ops, SparseCore 0:
  10.5 119.1 all-gather.3
  133.0 122.6 all-gather.5
  341.1 106.7 all-reduce.1
where the time goes:
time: 461 us; the launch traced here: 459 us
  waiting for transfers between devices  311 us (67%)
  local copies, waits for them, and re-layouts  77 us (17%)
  other arithmetic  33.3 us (7%)
  matrix products  24 us (5%)
  between operations  13.3 us (3%)
    all_gather x1, waiting for transfers between devices, turned_gather(): out = lax.all_gather(both, axis, axis=0, tiled=True)  107 us
    psum x1, waiting for transfers between devices, shards(): return lax.psum(partial_value.astype(jnp.bfloat16), 'tensor')  107 us
    all_gather x1, waiting for transfers between devices, side_by_side(): out = lax.all_gather(both, axis, axis=dim, tiled=True)  97.6 us
    unnamed x13, local copies, waits for them, and re-layouts  34 us
    mul x5, other arithmetic, dequant(): weight = blocks * factor  18.2 us
    reshape x2, local copies, waits for them, and re-layouts, side_by_side(): b.reshape(*out.shape[:along], *a.shape[along:])  14 us
    dot_general x3, matrix products, product(): jnp.dot(normed, dequant(blocks, scales), preferred_element_type=jnp.float32)  12.5 us
    dot_general x1, local copies, waits for them, and re-layouts, product(): jnp.dot(normed, dequant(blocks, scales), preferred_element_type=jnp.float32)  11.4 us
  transfers between devices with their start and end apart: 3, of which 3 were waited for; matrix products, arithmetic and copies ran while one was open for 9% of the time, Pallas kernels for 0%

commit v1 on v0

--- a/solution.py
+++ b/solution.py
@@ -1,40 +1,200 @@
+import functools
 import math
 
 import jax
 import jax.numpy as jnp
 from jax import lax
+from jax.experimental import pallas as pl
+from jax.experimental.pallas import tpu as pltpu
 from jax.sharding import PartitionSpec as P
 
 HEAD_DIM = 128
 SEQ = 256
-
-
 EPS = 1e-05
 ROPE_BASE = 500000.0
-
-
-def turned_gather(arrays, axis, dims):
-    turned = [jnp.moveaxis(a, dim, 0) for a, dim in zip(arrays, dims)]
-    widths = [t[0].size for t in turned]
-    both = jnp.concatenate([t.reshape(-1, w) for t, w in zip(turned, widths)], axis=1)
-    out = lax.all_gather(both, axis, axis=0, tiled=True)
-    blocks = jnp.split(out, [sum(widths[:k]) for k in range(1, len(widths))], axis=1)
-    return tuple(
-        (
-            jnp.moveaxis(b.reshape(-1, *t.shape[1:]), 0, dim)
-            for b, t, dim in zip(blocks, turned, dims)
+MESH = pl.DeviceIdType.MESH
+OFF = (0, -1, 1, 2)
+LAG = 3
+ROWS = 64
+
+
+def turn(v, d):
+    return lax.rem(v + (d + 4), 4)
+
+
+class Half:
+    def __init__(self, half, own, buf, recv, send, place):
+        self.half, self.own, self.buf, self.recv, self.sent = half, own, buf, recv, send
+        x, y, z = place
+        self.z = z
+        self.m, self.l = (x, y) if half == 0 else (y, x)
+        self.waited = {(0, 0, 0)}
+
+    def index(self, m, l, z):
+        return l * 16 + z * 4 + m if self.half == 0 else m * 16 + z * 4 + l
+
+    def slot(self, key):
+        r, jm, jl = key
+        return self.index(turn(self.m, OFF[jm]), turn(self.l, OFF[jl]), turn(self.z, OFF[r]))
+
+    def rows(self, key):
+        return self.buf.at[pl.ds(pl.multiple_of(self.slot(key) * ROWS, ROWS), ROWS)]
+
+    def copy(self, key, device):
+        src = self.own if key == (0, 0, 0) else self.rows(key)
+        return pltpu.make_async_remote_copy(
+            src_ref=src,
+            dst_ref=self.rows(key),
+            send_sem=self.sent,
+            recv_sem=self.recv.at[self.slot(key)],
+            device_id={"dp": device},
+            device_id_type=MESH,
         )
-    )
-
-
-def side_by_side(arrays, axis, dim, along):
-    widths = [math.prod(a.shape[along:]) for a in arrays]
-    both = jnp.concatenate(
-        [a.reshape(*a.shape[:along], w) for a, w in zip(arrays, widths)], axis=along
-    )
-    out = lax.all_gather(both, axis, axis=dim, tiled=True)
-    blocks = jnp.split(out, [sum(widths[:k]) for k in range(1, len(widths))], axis=along)
-    return tuple((b.reshape(*out.shape[:along], *a.shape[along:]) for a, b in zip(arrays, blocks)))
+
+    def near(self, dim, d):
+        m, l, z = self.m, self.l, self.z
+        if dim == "z":
+            z = turn(z, d)
+        elif dim == "m":
+            m = turn(m, d)
+        else:
+            l = turn(l, d)
+        return self.index(m, l, z)
+
+    def ensure(self, key):
+        if key not in self.waited:
+            self.waited.add(key)
+            self.copy(key, self.near("m", 1)).wait_recv()
+
+    def both(self, key, dim):
+        self.ensure(key)
+        self.copy(key, self.near(dim, 1)).start()
+        self.copy(key, self.near(dim, -1)).start()
+
+    def forward(self, key_minus, key_plus, dim, way):
+        if way % 2 == 0:
+            self.ensure(key_minus)
+            self.copy(key_minus, self.near(dim, 1)).start()
+        else:
+            self.ensure(key_plus)
+            self.copy(key_plus, self.near(dim, -1)).start()
+
+    def zed(self):
+        self.both((0, 0, 0), "z")
+
+    def zed_on(self):
+        self.forward((1, 0, 0), (2, 0, 0), "z", self.half)
+
+    def mid(self, r):
+        self.both((r, 0, 0), "m")
+
+    def mid_on(self, r):
+        self.forward((r, 1, 0), (r, 2, 0), "m", r)
+
+    def last(self, r, j):
+        self.both((r, j, 0), "l")
+
+    def last_on(self, r, j):
+        self.forward((r, j, 1), (r, j, 2), "l", j)
+
+    def done(self, r):
+        for j in range(4):
+            for k in range(4):
+                self.ensure((r, j, k))
+
+    def drain(self):
+        part = self.buf.at[pl.ds(0, 63 * ROWS)]
+        pltpu.make_async_remote_copy(
+            src_ref=part,
+            dst_ref=part,
+            send_sem=self.sent,
+            recv_sem=self.recv.at[0],
+            device_id={"dp": self.near("m", 1)},
+            device_id_type=MESH,
+        ).wait_send()
+
+
+def gather_kernel(qa_in, qb_in, oa_in, ob_in, qa, qb, oa, ob, recv, sent):
+    dp = lax.axis_index("dp")
+    x, z, y = lax.rem(dp, 4), lax.rem(dp // 4, 4), dp // 16
+    place = (x, y, z)
+    refs = (((qa_in, qa), (qb_in, qb)), ((oa_in, oa), (ob_in, ob)))
+    streams = [
+        [Half(h, *refs[s][h], recv.at[s, h], sent.at[s, h], place) for h in range(2)]
+        for s in range(2)
+    ]
+    first = streams[0][0]
+    barrier = pltpu.get_barrier_semaphore()
+    for dim in ("m", "l", "z"):
+        for d in (1, -1):
+            pl.semaphore_signal(
+                barrier, inc=1, device_id={"dp": first.near(dim, d)}, device_id_type=MESH
+            )
+    pl.semaphore_wait(barrier, 6)
+    for st in streams[0]:
+        st.last(0, 0)
+        st.mid(0)
+        st.zed()
+    for st in streams[0]:
+        st.mid_on(0)
+        st.zed_on()
+    for s in range(2):
+        for st in streams[s]:
+            slot = pl.ds(pl.multiple_of(dp * ROWS, ROWS), ROWS)
+            st.buf[slot, :] = st.own[...]
+
+    def on(i):
+        for st in streams[i // 16]:
+            st.last_on((i // 4) % 4, i % 4)
+
+    for i in range(32):
+        s, r, j = i // 16, (i // 4) % 4, i % 4
+        if i > 0:
+            for st in streams[s]:
+                st.last(r, j)
+        n = i // 4 + 1
+        if n < 8:
+            if j == 0:
+                for st in streams[n // 4]:
+                    st.mid(n % 4)
+            if j == 2:
+                for st in streams[n // 4]:
+                    st.mid_on(n % 4)
+        if i == 8:
+            for st in streams[1]:
+                st.zed()
+        if i == 10:
+            for st in streams[1]:
+                st.zed_on()
+        if i >= LAG:
+            on(i - LAG)
+    for i in range(32 - LAG, 32):
+        on(i)
+    for s in range(2):
+        for st in streams[s]:
+            for r in range(4):
+                st.done(r)
+    for s in range(2):
+        for st in streams[s]:
+            st.drain()
+
+
+def gather(qa, qb, oa, ob):
+    vmem = pl.BlockSpec(memory_space=pltpu.VMEM)
+    whole = [jax.ShapeDtypeStruct((64 * ROWS, a.shape[1]), a.dtype) for a in (qa, qb, oa, ob)]
+    return pl.pallas_call(
+        gather_kernel,
+        out_shape=whole,
+        in_specs=[vmem] * 4,
+        out_specs=[vmem] * 4,
+        scratch_shapes=[
+            pltpu.SemaphoreType.DMA((2, 2, 64)),
+            pltpu.SemaphoreType.DMA((2, 2)),
+        ],
+        compiler_params=pltpu.CompilerParams(
+            collective_id=0, has_side_effects=True, vmem_limit_bytes=60 * 2**20
+        ),
+    )(qa, qb, oa, ob)
 
 
 def dequant(blocks, scales):
@@ -95,27 +255,24 @@
     output_blocks,
     output_scales,
 ):
-    query_exps = query_scales.astype(jnp.bfloat16)
-    key_exps = key_scales.astype(jnp.bfloat16)
-    value_exps = value_scales.astype(jnp.bfloat16)
-    output_exps = output_scales.astype(jnp.bfloat16)
-    output_whole = turned_gather((output_blocks, output_exps), "dp", (2, 2))
+    query = dequant(query_blocks, query_scales)
+    key = dequant(key_blocks, key_scales)
+    value = dequant(value_blocks, value_scales)
+    output = dequant(output_blocks, output_scales).T
+    qa_in = jnp.concatenate([query[:, :512], key], axis=1)
+    qb_in = jnp.concatenate([query[:, 512:], value], axis=1)
+    qa, qb, oa, ob = gather(qa_in, qb_in, output[:, :512], output[:, 512:])
     wide_rows = activations.astype(jnp.float32)
     inverse = lax.rsqrt(jnp.mean(wide_rows * wide_rows, axis=-1, keepdims=True) + EPS)
     normed = (wide_rows * inverse * norm_gain.astype(jnp.float32)).astype(jnp.bfloat16)
-
-    def product(blocks, scales):
-        return jnp.dot(normed, dequant(blocks, scales), preferred_element_type=jnp.float32)
-
-    pieces = side_by_side(
-        (query_blocks, query_exps, key_blocks, key_exps, value_blocks, value_exps), "dp", 0, 1
-    )
-    query_states = product(pieces[0], pieces[1])
-    key_states = product(pieces[2], pieces[3])
-    value_states = product(pieces[4], pieces[5])
-    context = attend(query_states, key_states, value_states, key_blocks.shape[2] // HEAD_DIM)
-    partial_value = jnp.dot(
-        context, dequant(output_whole[0], output_whole[1]), preferred_element_type=jnp.float32
+    a = jnp.dot(normed, qa, preferred_element_type=jnp.float32)
+    b = jnp.dot(normed, qb, preferred_element_type=jnp.float32)
+    query_states = jnp.concatenate([a[:, :512], b[:, :512]], axis=1)
+    context = attend(query_states, a[:, 512:], b[:, 512:], 1)
+    partial_value = lax.dot_general(
+        context[:, :512], oa, (((1,), (1,)), ((), ())), preferred_element_type=jnp.float32
+    ) + lax.dot_general(
+        context[:, 512:], ob, (((1,), (1,)), ((), ())), preferred_element_type=jnp.float32
     )
     return lax.psum(partial_value.astype(jnp.bfloat16), "tensor")
 

time: 461 us -> 273 us (0.59)
  waiting for transfers between devices: 311 us -> 98.2 us
  Pallas kernels: 0 us -> 118 us
  local copies, waits for them, and re-layouts: 77 us -> 8.19 us
  other arithmetic: 33.3 us -> 11.8 us
    all_gather x2 -> x0, waiting for transfers between devices: 205 us -> none  [the longest x1 107 us: turned_gather(): out = lax.all_gather(both, axis, axis=0, tiled=True)]
    pallas_call x0 -> x1, Pallas kernels: none -> 118 us  [gather(): pl.pallas_call(gather_kernel, out_shape=whole, in_specs=[vmem] * 4, out_s...]
    unnamed x13 -> x19, local copies, waits for them, and re-layouts: 34 us -> 5.48 us
    mul x5 -> x4, other arithmetic: 18.2 us -> 1.91 us  [dequant(): weight = blocks * factor]
    split x2 -> x0, local copies, waits for them, and re-layouts: 15 us -> none  [the longest x1 7.67 us: turned_gather(): jnp.split(out, [sum(widths[:k]) for k in range(1, len(widths))], axis=1)]
    reshape x2 -> x1, local copies, waits for them, and re-layouts: 14 us -> 0.13 us  [dequant(): return weight.reshape(weight.shape[0] * weight.shape[1], weight.shape[2])]
    dot_general x1 -> x0, local copies, waits for them, and re-layouts: 11.4 us -> none  [product(): jnp.dot(normed, dequant(blocks, scales), preferred_element_type=jnp.float32)]
    psum x1, waiting for transfers between devices: 107 us -> 98.2 us  [shards(): return lax.psum(partial_value.astype(jnp.bfloat16), 'tensor')]
  transfers between devices with their start and end apart: 3 -> 1, of which waited for: 3 -> 1; matrix products, arithmetic and copies ran while one was open for 9% -> 0% of each run, Pallas kernels for 0% -> 0%
where the time goes in v1:
time: 273 us
  Pallas kernels  118 us (43%)
  waiting for transfers between devices  98.2 us (36%)
  matrix products  22.5 us (8%)
  between operations  13.7 us (5%)
  other arithmetic  11.8 us (4%)
  local copies, waits for them, and re-layouts  8.19 us (3%)
    pallas_call x1, Pallas kernels, gather(): pl.pallas_call(gather_kernel, out_shape=whole, in_specs=[vmem] * 4, out_s...  118 us
    psum x1, waiting for transfers between devices, shards(): return lax.psum(partial_value.astype(jnp.bfloat16), 'tensor')  98.2 us
    dot_general x1, matrix products, shards(): a = jnp.dot(normed, qa, preferred_element_type=jnp.float32)  7.22 us
    unnamed x19, local copies, waits for them, and re-layouts  5.48 us
  transfers between devices with their start and end apart: 1, of which 1 were waited for; matrix products, arithmetic and copies ran while one was open for 0% of the time, Pallas kernels for 0%

profile of v1, /device:TPU:1, one launch (start us, length us, event | category | flops | bytes accessed | tf_op | source)
XLA Modules:
  0.0 272.9 jit_solution(9000126188368596972)
XLA Ops:
  6.5 0.0 copy-start.3
  6.5 0.0 copy-start.4
  6.5 0.0 all-reduce.2.cloned.1.call-start
  6.6 0.7 exponential_convert_fusion.1
  7.3 0.9 broadcast_multiply_fusion.1
  8.2 0.7 exponential_convert_fusion.3
  8.9 0.7 exponential_convert_fusion.2
  9.6 0.8 exponential_convert_fusion
  10.4 1.0 broadcast_multiply_fusion
  11.4 0.1 copy.16
  11.5 0.6 fusion.33
  12.2 0.7 convert_element_type.79
  12.9 3.1 %fusion = f32[512]{0:T(512)S(1)} fusion(bf16[512,4096]{1,0:T(8,128)(2,1)} %param.10), kind=kLoop, calls=%fused_computation.2 | loop fusion | flops 6290944 | bytes 4196352 | tf_op jit(solution)/shard_map/reduce_sum | solution.py:266
  16.0 0.0 copy-done.3
  16.0 0.0 copy-done.4
  16.0 0.7 pad_maximum_fusion
  16.7 118.5 %shard_map.100 = (bf16[4096,640]{1,0:T(8,128)(2,1)}, bf16[4096,640]{1,0:T(8,128)(2,1)}, bf16[4096,512]{1,0:T(8,128)(2,1)}, bf16[4096,512]{1,0:T(8,128)(2,1)}) custom-call(bf16[64,640]{1,0:T(8,128)(2,1)} %get-tuple-element.27.qa_in, bf16[64,640]{1,0:T(8,128)(2,1)} %get-tuple-element.28.qb_in, bf16[64,512]{1,0:T(8,128)(2,1)} %get-tuple-element.20.oa_in, ...), custom_call_target="tpu_custom_call" | custom-call | tf_op jit(solution)/shard_map/pallas_call | solution.py:185
  135.2 0.0 copy-start
  135.2 0.0 copy-start.5
  135.2 7.2 %fusion.14 = f32[512,640]{1,0:T(8,128)S(1)} fusion(bf16[4096,640]{1,0:T(8,128)(2,1)} %get-tuple-element.10, bf16[512,4096]{1,0:T(8,128)(2,1)} %param.10, f32[4096]{0:T(1024)S(1)} %convert_element_type.79, f32[512]{0:T(512)S(1)} %add_rsqrt_fusion), kind=kOutput, calls=%fused_computation.19 | convolution fusion | flops 2692743168 | bytes 10766336 | tf_op jit(solution)/shard_map/dot_general | solution.py:268
  142.4 0.0 copy-start.2
  142.4 0.1 slice.65
  142.6 0.0 copy-done
  142.6 0.0 copy-done.5
  142.6 3.5 %fusion.16 = f32[512,640]{1,0:T(8,128)S(1)} fusion(bf16[4096,640]{1,0:T(8,128)(2,1)S(1)} %copy-done.5, bf16[512,4096]{1,0:T(8,128)(2,1)S(1)} %copy-done, f32[4096]{0:T(1024)S(1)} %convert_element_type.79, f32[512]{0:T(512)S(1)} %add_rsqrt_fusion), kind=kOutput, calls=%fused_computation.20 | convolution fusion | flops 2692743168 | bytes 10766336 | tf_op jit(solution)/shard_map/dot_general | solution.py:269
  146.1 0.0 copy-done.2
  146.1 0.1 slice.66
  146.3 0.2 maximum_bitcast_fusion
  146.4 0.5 copy.33
  146.9 0.0 slice-start
  146.9 0.7 fusion.32
  147.6 0.5 multiply_cosine_fusion
  148.1 0.0 slice-done
  148.1 0.2 fusion.25
  148.3 0.8 subtract_convert_fusion
  149.1 1.4 fusion.4
  150.5 0.9 fusion.3
  151.4 1.3 fusion.11
  152.7 1.0 copy.21
  153.7 0.3 copy.44
  153.9 0.0 copy-start.1
  153.9 4.7 %fusion.23 = f32[512,4096]{1,0:T(8,128)S(1)} fusion(bf16[4096,512]{1,0:T(8,128)(2,1)} %get-tuple-element.11, bf16[512,1024]{1,0:T(8,128)(2,1)S(1)} %bitcast.78), kind=kOutput, calls=%fused_computation.27 | convolution fusion | flops 2147483648 | bytes 13107200 | tf_op jit(solution)/shard_map/dot_general | solution.py:272
  158.7 0.0 copy-done.1
  158.7 4.4 %add_convert_fusion = bf16[512,4096]{1,0:T(8,128)(2,1)} fusion(f32[512,4096]{1,0:T(8,128)S(1)} %fusion.23, bf16[4096,512]{1,0:T(8,128)(2,1)S(1)} %copy-done.1, bf16[512,1024]{1,0:T(8,128)(2,1)S(1)} %bitcast.79), kind=kOutput, calls=%fused_computation.5 | convolution fusion | flops 2151677952 | bytes 17301504 | tf_op jit(solution)/shard_map/dot_general | solution.py:274
  163.1 0.0 all-reduce.2.cloned.1.call-update
  163.1 98.2 %all-reduce.2.cloned.1.call-done = bf16[512,4096]{1,0:T(8,128)(2,1)} async-done(((bf16[512,4096]{1,0:T(8,128)(2,1)}), bf16[512,4096]{1,0:T(8,128)(2,1)}) %all-reduce.2.cloned.1.call-update) | async-done | bytes 4194320 | tf_op jit(solution)/shard_map/psum | solution.py:277
  261.3 4.7 %copy.50 = bf16[512,4096]{1,0:T(8,128)(2,1)} copy(bf16[512,4096]{1,0:T(8,128)(2,1)} %all-reduce.2.cloned.1.call-done) | data formatting | bytes 8388608
  (12 shorter events, 0.1 us)
Async XLA Ops:
  6.5 9.4 %copy-start.3 = (bf16[2,32,128]{2,1,0:T(8,128)(2,1)S(1)}, bf16[2,32,128]{2,1,0:T(8,128)(2,1)}, u32[]{:S(2)}) copy-start(bf16[2,32,128]{2,1,0:T(8,128)(2,1)} %param.14) | copy-start | bytes 49156
  6.5 9.4 %copy-start.4 = (bf16[2,32,128]{2,1,0:T(8,128)(2,1)S(1)}, bf16[2,32,128]{2,1,0:T(8,128)(2,1)}, u32[]{:S(2)}) copy-start(bf16[2,32,128]{2,1,0:T(8,128)(2,1)} %param.16) | copy-start | bytes 49156
  6.5 254.8 %all-reduce.2.cloned.1.call-start = ((), (), s32[]{:S(2)}) async-start(), calls=%async_computation | async-start | bytes 8388608 | tf_op jit(solution)/shard_map/psum | solution.py:277
  135.2 7.4 %copy-start = (bf16[512,4096]{1,0:T(8,128)(2,1)S(1)}, bf16[512,4096]{1,0:T(8,128)(2,1)}, u32[]{:S(2)}) copy-start(bf16[512,4096]{1,0:T(8,128)(2,1)} %param.10) | copy-start | bytes 12582916
  135.2 7.4 %copy-start.5 = (bf16[4096,640]{1,0:T(8,128)(2,1)S(1)}, bf16[4096,640]{1,0:T(8,128)(2,1)}, u32[]{:S(2)}) copy-start(bf16[4096,640]{1,0:T(8,128)(2,1)} %get-tuple-element.9) | copy-start | bytes 15728644
  142.4 3.7 %copy-start.2 = (f32[512,640]{1,0:T(8,128)}, f32[512,640]{1,0:T(8,128)S(1)}, u32[]{:S(2)}) copy-start(f32[512,640]{1,0:T(8,128)S(1)} %fusion.14) | copy-start | bytes 3932164
  146.9 1.2 slice-start
  153.9 4.7 %copy-start.1 = (bf16[4096,512]{1,0:T(8,128)(2,1)S(1)}, bf16[4096,512]{1,0:T(8,128)(2,1)}, u32[]{:S(2)}) copy-start(bf16[4096,512]{1,0:T(8,128)(2,1)} %get-tuple-element.12) | copy-start | bytes 12582916
Sparse Core Ops, SparseCore 0:
  163.3 98.0 all-reduce.1

commit v2 on v1

v2 whole, which is shorter than its diff:
```python
import math

import jax
import jax.numpy as jnp
import numpy as np
from jax import lax
from jax.experimental import pallas as pl
from jax.experimental.pallas import tpu as pltpu
from jax.sharding import PartitionSpec as P

HEAD_DIM = 128
SEQ = 256
EPS = 1e-05
ROPE_BASE = 500000.0
MESH = pl.DeviceIdType.MESH
OFF = (0, -1, 1, 2)
LAG = 3
ROWS = 64


def turn(v, d):
    return lax.rem(v + (d + 4), 4)


class Half:
    def __init__(self, half, buf, recv, send, place):
        self.half, self.buf, self.recv, self.sent = half, buf, recv, send
        x, y, z = place
        self.z = z
        self.m, self.l = (x, y) if half == 0 else (y, x)
        self.waited = {(0, 0, 0)}

    def index(self, m, l, z):
        return l * 16 + z * 4 + m if self.half == 0 else m * 16 + z * 4 + l

    def slot(self, key):
        r, jm, jl = key
        return self.index(turn(self.m, OFF[jm]), turn(self.l, OFF[jl]), turn(self.z, OFF[r]))

    def rows(self, key):
        return self.buf.at[pl.ds(pl.multiple_of(self.slot(key) * ROWS, ROWS), ROWS)]

    def copy(self, key, device):
        return pltpu.make_async_remote_copy(
            src_ref=self.rows(key),
            dst_ref=self.rows(key),
            send_sem=self.sent,
            recv_sem=self.recv.at[self.slot(key)],
            device_id={"dp": device},
            device_id_type=MESH,
        )

    def near(self, dim, d):
        m, l, z = self.m, self.l, self.z
        if dim == "z":
            z = turn(z, d)
        elif dim == "m":
            m = turn(m, d)
        else:
            l = turn(l, d)
        return self.index(m, l, z)

    def ensure(self, key):
        if key not in self.waited:
            self.waited.add(key)
            self.copy(key, self.near("m", 1)).wait_recv()

    def both(self, key, dim):
        self.ensure(key)
        self.copy(key, self.near(dim, 1)).start()
        self.copy(key, self.near(dim, -1)).start()

    def forward(self, key_minus, key_plus, dim, way):
        if way % 2 == 0:
            self.ensure(key_minus)
            self.copy(key_minus, self.near(dim, 1)).start()
        else:
            self.ensure(key_plus)
            self.copy(key_plus, self.near(dim, -1)).start()

    def zed(self):
        self.both((0, 0, 0), "z")

    def zed_on(self):
        self.forward((1, 0, 0), (2, 0, 0), "z", self.half)

    def mid(self, r):
        self.both((r, 0, 0), "m")

    def mid_on(self, r):
        self.forward((r, 1, 0), (r, 2, 0), "m", r)

    def last(self, r, j):
        self.both((r, j, 0), "l")

    def last_on(self, r, j):
        self.forward((r, j, 1), (r, j, 2), "l", j)

    def done(self, r):
        for j in range(4):
            for k in range(4):
                self.ensure((r, j, k))

    def drain(self):
        part = self.buf.at[pl.ds(0, 63 * ROWS)]
        pltpu.make_async_remote_copy(
            src_ref=part,
            dst_ref=part,
            send_sem=self.sent,
            recv_sem=self.recv.at[0],
            device_id={"dp": self.near("m", 1)},
            device_id_type=MESH,
        ).wait_send()


def product(a, b):
    return jnp.dot(a, b, preferred_element_type=jnp.float32)


def product_t(a, b):
    return lax.dot_general(a, b, (((1,), (1,)), ((), ())), preferred_element_type=jnp.float32)


def layer_kernel(
    act_in,
    gain,
    cosine,
    sine,
    qa_in,
    qb_in,
    oa_in,
    ob_in,
    out,
    act,
    qa,
    qb,
    oa,
    ob,
    acc_a,
    acc_b,
    keys,
    values,
    context,
    give,
    keep,
    got,
    pair,
    over,
    total,
    recv,
    sent,
    sum_recv,
    sum_sent,
    io,
):
    dp = lax.axis_index("dp")
    tensor = lax.axis_index("tensor")
    x, z, y = lax.rem(dp, 4), lax.rem(dp // 4, 4), dp // 16
    core = lax.rem(tensor, 2)
    sibling = tensor + 1 - 2 * core
    partner = lax.rem(tensor + 2, 4)
    mine = pl.ds(pl.multiple_of(core * SEQ, SEQ), SEQ)
    other = pl.ds(pl.multiple_of((1 - core) * SEQ, SEQ), SEQ)
    slot = pl.ds(pl.multiple_of(dp * ROWS, ROWS), ROWS)
    bufs = ((qa, qb), (oa, ob))
    streams = [
        [Half(h, bufs[s][h], recv.at[s, h], sent.at[s, h], (x, y, z)) for h in range(2)]
        for s in range(2)
    ]
    first = streams[0][0]
    loads = [
        pltpu.make_async_copy(src, dst.at[slot], io.at[k])
        for k, (src, dst) in enumerate(((qa_in, qa), (qb_in, qb), (oa_in, oa), (ob_in, ob)))
    ]
    load_act = pltpu.make_async_copy(act_in, act, io.at[4])
    for load in loads:
        load.start()
    load_act.start()
    barrier = pltpu.get_barrier_semaphore()
    for dim in ("m", "l", "z"):
        for d in (1, -1):
            pl.semaphore_signal(
                barrier, inc=1, device_id={"dp": first.near(dim, d)}, device_id_type=MESH
            )
    for peer in (sibling, partner):
        pl.semaphore_signal(barrier, inc=1, device_id={"tensor": peer}, device_id_type=MESH)
    pl.semaphore_wait(barrier, 8)
    loads[0].wait()
    loads[1].wait()
    for st in streams[0]:
        st.last(0, 0)
        st.mid(0)
        st.zed()
    for st in streams[0]:
        st.mid_on(0)
        st.zed_on()
    loads[2].wait()
    loads[3].wait()
    acc_a[...] = jnp.zeros_like(acc_a)
    acc_b[...] = jnp.zeros_like(acc_b)
    load_act.wait()

    def norm(k):
        @pl.loop(0, 8)
        def _(i):
            rows = pl.ds(pl.multiple_of(k * 128 + i * 16, 16), 16)
            wide = act[rows, :].astype(jnp.float32)
            mean = jnp.mean(wide * wide, axis=-1, keepdims=True)
            scaled = wide * lax.rsqrt(mean + EPS) * gain[...].astype(jnp.float32)
            act[rows, :] = scaled.astype(jnp.bfloat16)

    def project(r):
        for st in streams[0]:
            st.done(r)
        zs = turn(z, OFF[r])

        @pl.loop(0, 4)
        def _(k):
            part = pl.ds(pl.multiple_of((k * 4 + zs) * 256, 256), 256)
            acc_a[...] += product(act[:, part], qa[part, :])
            acc_b[...] += product(act[:, part], qb[part, :])

    def rotate(states):
        return states * cosine[...] + pltpu.roll(states, HEAD_DIM // 2, 1) * sine[...]

    def keys_values(s):
        rows = pl.ds(s * SEQ, SEQ)
        keys[rows, :] = rotate(acc_a[rows, 512:]).astype(jnp.bfloat16)
        values[rows, :] = acc_b[rows, 512:].astype(jnp.bfloat16)

    def attend(s, h):
        rows = pl.ds(s * SEQ, SEQ)
        acc = (acc_a, acc_b)[h]

        @pl.loop(0, 4)
        def _(k):
            head = pl.ds(pl.multiple_of(k * HEAD_DIM, HEAD_DIM), HEAD_DIM)
            queries = rotate(acc[rows, head]).astype(jnp.bfloat16)
            scores = product_t(queries, keys[rows, :]) * HEAD_DIM ** (-0.5)
            spot = lax.broadcasted_iota(jnp.int32, (SEQ, SEQ), 0)
            seen = lax.broadcasted_iota(jnp.int32, (SEQ, SEQ), 1)
            scores = jnp.where(spot >= seen, scores, -jnp.inf)
            raised = jnp.exp(scores - jnp.max(scores, axis=-1, keepdims=True))
            weights = raised * (1.0 / jnp.sum(raised, axis=-1, keepdims=True))
            wide = product(weights.astype(jnp.bfloat16), values[rows, :])
            place = pl.ds(pl.multiple_of(h * 512 + k * HEAD_DIM, HEAD_DIM), HEAD_DIM)
            context[rows, place] = wide.astype(jnp.bfloat16)

    def block(n):
        return lax.rem(n, 4) * 4 + turn(z, OFF[n // 4])

    def tensor_copy(stage, n, src, dst, peer):
        c = block(n)
        return pltpu.make_async_remote_copy(
            src_ref=src,
            dst_ref=dst,
            send_sem=sum_sent.at[stage],
            recv_sem=sum_recv.at[stage, c],
            device_id={"tensor": peer},
            device_id_type=MESH,
        )

    def hand(n):
        c = block(n)
        return tensor_copy(0, n, give.at[c], got.at[c], sibling)

    def cross(n):
        c = block(n)
        return tensor_copy(1, n, pair.at[c], over.at[c], partner)

    def share(n):
        c = block(n)
        return tensor_copy(2, n, total.at[c, mine], total.at[c, mine], sibling)

    def share_in(n):
        c = block(n)
        return tensor_copy(2, n, total.at[c, other], total.at[c, other], sibling)

    def put(n, half):
        c = block(n)
        columns = pl.ds(pl.multiple_of(c * 256, 256), 256)
        return pltpu.make_async_copy(total.at[c, half], out.at[half, columns], io.at[5])

    def partial(n, rows):
        part = pl.ds(pl.multiple_of(block(n) * 256, 256), 256)
        wide = product_t(context[rows, :512], oa[part, :]) + product_t(
            context[rows, 512:], ob[part, :]
        )
        return wide.astype(jnp.bfloat16)

    def pairs(n):
        c = block(n)
        hand(n).wait_recv()
        wide = keep[c].astype(jnp.float32) + got[c].astype(jnp.float32)
        pair[c] = wide.astype(jnp.bfloat16)

    def totals(n):
        c = block(n)
        cross(n).wait_recv()
        wide = pair[c].astype(jnp.float32) + over[c].astype(jnp.float32)
        total[c, mine, :] = wide.astype(jnp.bfloat16)

    def step(n):
        if n < 16 and n % 4 == 0:
            for st in streams[1]:
                st.done(n // 4)
        two, three, four = n - 1, n - 3, n - 4
        if 0 <= two < 16:
            pairs(two)
        if 0 <= three < 16:
            totals(three)
        if n < 16:
            give[block(n)] = partial(n, other)
        if 0 <= two < 16:
            cross(two).start()
        if 0 <= three < 16:
            share(three).start()
            put(three, mine).start()
        if 0 <= four < 16:
            share_in(four).wait_recv()
            put(four, other).start()
        if n < 16:
            keep[block(n)] = partial(n, mine)
            hand(n).start()

    def on(i):
        for st in streams[i // 16]:
            st.last_on((i // 4) % 4, i % 4)

    work = {i: [lambda k=i: norm(k)] for i in range(4)}
    for r in range(3):
        work.setdefault(4 * r + 7, []).append(lambda k=r: project(k))
    work[18] = [lambda: project(3), lambda: keys_values(0), lambda: keys_values(1)]
    work[19] = [lambda: attend(0, 0), lambda: attend(0, 1)]
    work[20] = [lambda: attend(1, 0), lambda: attend(1, 1)]
    for n, o in enumerate((6, 6, 7, 8, 10, 11, 12, 13, 14, 15)):
        work.setdefault(16 + o, []).append(lambda k=n: step(k))

    for i in range(32):
        s, r, j = i // 16, (i // 4) % 4, i % 4
        if i > 0:
            for st in streams[s]:
                st.last(r, j)
        n = i // 4 + 1
        if n < 8:
            if j == 0:
                for st in streams[n // 4]:
                    st.mid(n % 4)
            if j == 2:
                for st in streams[n // 4]:
                    st.mid_on(n % 4)
        if i == 8:
            for st in streams[1]:
                st.zed()
        if i == 10:
            for st in streams[1]:
                st.zed_on()
        if i >= LAG:
            on(i - LAG)
        for task in work.get(i, ()):
            task()
    for i in range(32 - LAG, 32):
        on(i)
    for n in range(10, 20):
        step(n)
    for s in range(2):
        for st in streams[s]:
            st.drain()
    for stage, ref in enumerate((give, pair, total.at[:, :SEQ])):
        pltpu.make_async_remote_copy(
            src_ref=ref,
            dst_ref=ref,
            send_sem=sum_sent.at[stage],
            recv_sem=sum_recv.at[stage, 0],
            device_id={"tensor": sibling},
            device_id_type=MESH,
        ).wait_send()
    pltpu.make_async_copy(out, out, io.at[5]).wait()


def tables():
    half = HEAD_DIM // 2
    frequency = np.exp(-math.log(ROPE_BASE) * np.arange(half) * 2.0 / HEAD_DIM)
    angles = np.arange(SEQ)[:, None] * frequency[None, :]
    cosine, sine = np.cos(angles), np.sin(angles)
    return (
        np.concatenate([cosine, cosine], axis=1).astype(np.float32),
        np.concatenate([-sine, sine], axis=1).astype(np.float32),
    )


def layer(activations, gain, qa, qb, oa, ob):
    vmem = pl.BlockSpec(memory_space=pltpu.VMEM)
    hbm = pl.BlockSpec(memory_space=pltpu.HBM)
    tokens, features = activations.shape
    cosine, sine = tables()
    kind = jnp.bfloat16
    chunks = features // 256
    return pl.pallas_call(
        layer_kernel,
        out_shape=jax.ShapeDtypeStruct((tokens, features), kind),
        in_specs=[hbm, vmem, vmem, vmem, hbm, hbm, hbm, hbm],
        out_specs=hbm,
        scratch_shapes=[
            pltpu.VMEM((tokens, features), kind),
            pltpu.VMEM((features, 640), kind),
            pltpu.VMEM((features, 640), kind),
            pltpu.VMEM((features, 512), kind),
            pltpu.VMEM((features, 512), kind),
            pltpu.VMEM((tokens, 640), jnp.float32),
            pltpu.VMEM((tokens, 640), jnp.float32),
            pltpu.VMEM((tokens, HEAD_DIM), kind),
            pltpu.VMEM((tokens, HEAD_DIM), kind),
            pltpu.VMEM((tokens, 1024), kind),
            pltpu.VMEM((chunks, SEQ, 256), kind),
            pltpu.VMEM((chunks, SEQ, 256), kind),
            pltpu.VMEM((chunks, SEQ, 256), kind),
            pltpu.VMEM((chunks, SEQ, 256), kind),
            pltpu.VMEM((chunks, SEQ, 256), kind),
            pltpu.VMEM((chunks, tokens, 256), kind),
            pltpu.SemaphoreType.DMA((2, 2, 64)),
            pltpu.SemaphoreType.DMA((2, 2)),
            pltpu.SemaphoreType.DMA((3, 16)),
            pltpu.SemaphoreType.DMA((3,)),
            pltpu.SemaphoreType.DMA((6,)),
        ],
        compiler_params=pltpu.CompilerParams(
            collective_id=0, has_side_effects=True, vmem_limit_bytes=60 * 2**20
        ),
    )(activations, gain, cosine, sine, qa, qb, oa, ob)


def dequant(blocks, scales):
    factor = jnp.exp2(scales.astype(jnp.float32)).astype(blocks.dtype)
    weight = blocks * factor
    return weight.reshape(weight.shape[0] * weight.shape[1], weight.shape[2])


def shards(
    activations,
    norm_gain,
    query_blocks,
    query_scales,
    key_blocks,
    key_scales,
    value_blocks,
    value_scales,
    output_blocks,
    output_scales,
):
    query = dequant(query_blocks, query_scales)
    key = dequant(key_blocks, key_scales)
    value = dequant(value_blocks, value_scales)
    output = dequant(output_blocks, output_scales).T
    qa = jnp.concatenate([query[:, :512], key], axis=1)
    qb = jnp.concatenate([query[:, 512:], value], axis=1)
    return layer(
        activations, norm_gain.reshape(1, -1), qa, qb, output[:, :512], output[:, 512:]
    )


def solution(mesh):
    placed = (
        P("dp", None),
        P(),
        P("dp", None, "tensor"),
        P("dp", None, "tensor"),
        P("dp", None, "tensor"),
        P("dp", None, "tensor"),
        P("dp", None, "tensor"),
        P("dp", None, "tensor"),
        P("tensor", None, "dp"),
        P("tensor", None, "dp"),
    )
    return jax.shard_map(
        shards, mesh=mesh, in_specs=placed, out_specs=P("dp", None), check_vma=False
    )
```

time: 273 us -> 175 us (0.64)
  waiting for transfers between devices: 98.2 us -> 0 us
  Pallas kernels: 118 us -> 160 us
  matrix products: 22.5 us -> 0 us
  between operations: 13.7 us -> 0.06 us
  other arithmetic: 11.8 us -> 6.84 us
    psum x1 -> x0, waiting for transfers between devices: 98.2 us -> none  [shards(): return lax.psum(partial_value.astype(jnp.bfloat16), 'tensor')]
    pallas_call x1, Pallas kernels: 118 us -> 160 us  [layer(): pl.pallas_call(layer_kernel, out_shape=jax.ShapeDtypeStruct((tokens, feat...]
    dot_general x6 -> x0, matrix products: 22.5 us -> none  [the longest x1 7.22 us: shards(): a = jnp.dot(normed, qa, preferred_element_type=jnp.float32)]
    reduce_sum x2 -> x0, other arithmetic: 3.95 us -> none  [the longest x1 3.08 us: shards(): jnp.mean(wide_rows * wide_rows, axis=-1, keepdims=True) + EPS]
    unnamed x19 -> x5, local copies, waits for them, and re-layouts: 5.48 us -> 4.72 us
  transfers between devices with their start and end apart: 1 -> 0, of which waited for: 1 -> 0; matrix products, arithmetic and copies ran while one was open for 0% -> 0% of each run, Pallas kernels for 0% -> 0%
where the time goes in v2:
time: 175 us; the launch traced here: 174 us
  Pallas kernels  160 us (91%)
  other arithmetic  6.84 us (4%)
  local copies, waits for them, and re-layouts  6.81 us (4%)
    pallas_call x1, Pallas kernels, layer(): pl.pallas_call(layer_kernel, out_shape=jax.ShapeDtypeStruct((tokens, feat...  160 us
    unnamed x5, local copies, waits for them, and re-layouts  4.72 us

profile of v2, /device:TPU:1, one launch (start us, length us, event | category | flops | bytes accessed | tf_op | source)
XLA Modules:
  0.0 174.0 jit_solution(17607087974482313937)
XLA Ops:
  0.0 0.7 exponential_convert_fusion.3
  0.7 0.7 exponential_convert_fusion.2
  1.4 0.7 exponential_convert_fusion.1
  2.1 0.7 broadcast_multiply_fusion.2
  2.9 0.7 broadcast_multiply_fusion.3
  3.6 1.3 reshape.15.gain
  4.9 0.7 exponential_convert_fusion
  5.6 0.9 broadcast_multiply_fusion.1
  6.6 0.7 pad_maximum_fusion
  7.2 1.0 broadcast_multiply_fusion
  8.2 0.1 copy.14
  8.4 0.6 fusion
  9.0 160.3 %shard_map.118 = bf16[512,4096]{1,0:T(8,128)(2,1)} custom-call(bf16[512,4096]{1,0:T(8,128)(2,1)} %act_in.1, bf16[1,4096]{1,0:T(2,128)(2,1)} %reshape.15.gain, f32[256,128]{1,0:T(8,128)} %constant.4.clone.cosine, f32[256,128]{1,0:T(8,128)} %constant.2.clone.sine, bf16[64,640]{1,0:T(8,128)(2,1)} %get-tuple-element.9.qa_in, ...), custom_call_target="tpu_custom_call" | custom-call | tf_op jit(solution)/shard_map/pallas_call | solution.py:399
  169.3 4.7 %copy.28 = bf16[512,4096]{1,0:T(8,128)(2,1)} copy(bf16[512,4096]{1,0:T(8,128)(2,1)} %shard_map.118) | data formatting | bytes 8388608
  (5 shorter events, 0.0 us)

commit v3 on v2

--- a/solution.py
+++ b/solution.py
@@ -14,7 +14,6 @@
 ROPE_BASE = 500000.0
 MESH = pl.DeviceIdType.MESH
 OFF = (0, -1, 1, 2)
-LAG = 3
 ROWS = 64
 
 
@@ -95,11 +94,6 @@
 
     def last_on(self, r, j):
         self.forward((r, j, 1), (r, j, 2), "l", j)
-
-    def done(self, r):
-        for j in range(4):
-            for k in range(4):
-                self.ensure((r, j, k))
 
     def drain(self):
         part = self.buf.at[pl.ds(0, 63 * ROWS)]
@@ -126,10 +120,14 @@
     gain,
     cosine,
     sine,
-    qa_in,
-    qb_in,
-    oa_in,
-    ob_in,
+    query_in,
+    query_exp,
+    key_in,
+    key_exp,
+    value_in,
+    value_exp,
+    output_in,
+    output_exp,
     out,
     act,
     qa,
@@ -147,6 +145,8 @@
     pair,
     over,
     total,
+    gain_row,
+    flat,
     recv,
     sent,
     sum_recv,
@@ -161,20 +161,13 @@
     partner = lax.rem(tensor + 2, 4)
     mine = pl.ds(pl.multiple_of(core * SEQ, SEQ), SEQ)
     other = pl.ds(pl.multiple_of((1 - core) * SEQ, SEQ), SEQ)
-    slot = pl.ds(pl.multiple_of(dp * ROWS, ROWS), ROWS)
     bufs = ((qa, qb), (oa, ob))
     streams = [
         [Half(h, bufs[s][h], recv.at[s, h], sent.at[s, h], (x, y, z)) for h in range(2)]
         for s in range(2)
     ]
     first = streams[0][0]
-    loads = [
-        pltpu.make_async_copy(src, dst.at[slot], io.at[k])
-        for k, (src, dst) in enumerate(((qa_in, qa), (qb_in, qb), (oa_in, oa), (ob_in, ob)))
-    ]
-    load_act = pltpu.make_async_copy(act_in, act, io.at[4])
-    for load in loads:
-        load.start()
+    load_act = pltpu.make_async_copy(act_in, act, io.at[0])
     load_act.start()
     barrier = pltpu.get_barrier_semaphore()
     for dim in ("m", "l", "z"):
@@ -184,21 +177,32 @@
             )
     for peer in (sibling, partner):
         pl.semaphore_signal(barrier, inc=1, device_id={"tensor": peer}, device_id_type=MESH)
+
+    def factor(exponents):
+        return jnp.exp2(exponents.astype(jnp.float32)).astype(jnp.bfloat16)
+
+    for b in range(2):
+        rows = pl.ds(pl.multiple_of(dp * ROWS + b * 32, 32), 32)
+        query = query_in[b] * factor(query_exp[b])
+        qa[rows, :512] = query[:, :512]
+        qb[rows, :512] = query[:, 512:]
+        qa[rows, 512:] = key_in[b] * factor(key_exp[b])
+        qb[rows, 512:] = value_in[b] * factor(value_exp[b])
+
+    def fill_output():
+        for b in range(32):
+            flat[b * 32 : (b + 1) * 32, :] = output_in[b] * factor(output_exp[b])
+        rows = pl.ds(pl.multiple_of(dp * ROWS, ROWS), ROWS)
+        oa[rows, :] = flat[:512, :].T
+        ob[rows, :] = flat[512:, :].T
+
+    def fill_gain():
+        for k in range(32):
+            gain_row[:, k * 128 : (k + 1) * 128] = gain[k : k + 1, :].astype(jnp.float32)
+        acc_a[...] = jnp.zeros_like(acc_a)
+        acc_b[...] = jnp.zeros_like(acc_b)
+
     pl.semaphore_wait(barrier, 8)
-    loads[0].wait()
-    loads[1].wait()
-    for st in streams[0]:
-        st.last(0, 0)
-        st.mid(0)
-        st.zed()
-    for st in streams[0]:
-        st.mid_on(0)
-        st.zed_on()
-    loads[2].wait()
-    loads[3].wait()
-    acc_a[...] = jnp.zeros_like(acc_a)
-    acc_b[...] = jnp.zeros_like(acc_b)
-    load_act.wait()
 
     def norm(k):
         @pl.loop(0, 8)
@@ -206,17 +210,25 @@
             rows = pl.ds(pl.multiple_of(k * 128 + i * 16, 16), 16)
             wide = act[rows, :].astype(jnp.float32)
             mean = jnp.mean(wide * wide, axis=-1, keepdims=True)
-            scaled = wide * lax.rsqrt(mean + EPS) * gain[...].astype(jnp.float32)
+            scaled = wide * lax.rsqrt(mean + EPS) * gain_row[...]
             act[rows, :] = scaled.astype(jnp.bfloat16)
 
-    def project(r):
-        for st in streams[0]:
-            st.done(r)
+    def need(s, r, k):
+        for j in range(4):
+            streams[s][0].ensure((r, j, k))
+        for j in range(4):
+            streams[s][1].ensure((r, k, j))
+
+    def project(r, parts):
+        for k in parts:
+            need(0, r, k)
         zs = turn(z, OFF[r])
 
-        @pl.loop(0, 4)
+        @pl.loop(parts[0], parts[-1] + 1)
         def _(k):
-            part = pl.ds(pl.multiple_of((k * 4 + zs) * 256, 256), 256)
+            away = 3 * k + 3 * (k // 2) + 2 * (k // 3)
+            spot = lax.rem(y + away, 4) * 4 + zs
+            part = pl.ds(pl.multiple_of(spot * 256, 256), 256)
             acc_a[...] += product(act[:, part], qa[part, :])
             acc_b[...] += product(act[:, part], qb[part, :])
 
@@ -228,26 +240,27 @@
         keys[rows, :] = rotate(acc_a[rows, 512:]).astype(jnp.bfloat16)
         values[rows, :] = acc_b[rows, 512:].astype(jnp.bfloat16)
 
-    def attend(s, h):
-        rows = pl.ds(s * SEQ, SEQ)
+    def attend(h):
         acc = (acc_a, acc_b)[h]
 
-        @pl.loop(0, 4)
-        def _(k):
-            head = pl.ds(pl.multiple_of(k * HEAD_DIM, HEAD_DIM), HEAD_DIM)
-            queries = rotate(acc[rows, head]).astype(jnp.bfloat16)
-            scores = product_t(queries, keys[rows, :]) * HEAD_DIM ** (-0.5)
+        @pl.loop(0, 2)
+        def _(s):
+            rows = pl.ds(pl.multiple_of(s * SEQ, SEQ), SEQ)
             spot = lax.broadcasted_iota(jnp.int32, (SEQ, SEQ), 0)
             seen = lax.broadcasted_iota(jnp.int32, (SEQ, SEQ), 1)
-            scores = jnp.where(spot >= seen, scores, -jnp.inf)
-            raised = jnp.exp(scores - jnp.max(scores, axis=-1, keepdims=True))
-            weights = raised * (1.0 / jnp.sum(raised, axis=-1, keepdims=True))
-            wide = product(weights.astype(jnp.bfloat16), values[rows, :])
-            place = pl.ds(pl.multiple_of(h * 512 + k * HEAD_DIM, HEAD_DIM), HEAD_DIM)
-            context[rows, place] = wide.astype(jnp.bfloat16)
+            for k in range(4):
+                queries = rotate(acc[rows, k * HEAD_DIM : (k + 1) * HEAD_DIM])
+                scores = product_t(queries.astype(jnp.bfloat16), keys[rows, :])
+                scores = scores * HEAD_DIM ** (-0.5)
+                scores = jnp.where(spot >= seen, scores, -jnp.inf)
+                raised = jnp.exp(scores - jnp.max(scores, axis=-1, keepdims=True))
+                weights = raised * (1.0 / jnp.sum(raised, axis=-1, keepdims=True))
+                wide = product(weights.astype(jnp.bfloat16), values[rows, :])
+                place = h * 512 + k * HEAD_DIM
+                context[rows, place : place + HEAD_DIM] = wide.astype(jnp.bfloat16)
 
     def block(n):
-        return lax.rem(n, 4) * 4 + turn(z, OFF[n // 4])
+        return turn(y, OFF[n % 4]) * 4 + turn(z, OFF[n // 4])
 
     def tensor_copy(stage, n, src, dst, peer):
         c = block(n)
@@ -279,7 +292,7 @@
     def put(n, half):
         c = block(n)
         columns = pl.ds(pl.multiple_of(c * 256, 256), 256)
-        return pltpu.make_async_copy(total.at[c, half], out.at[half, columns], io.at[5])
+        return pltpu.make_async_copy(total.at[c, half], out.at[half, columns], io.at[1])
 
     def partial(n, rows):
         part = pl.ds(pl.multiple_of(block(n) * 256, 256), 256)
@@ -301,9 +314,8 @@
         total[c, mine, :] = wide.astype(jnp.bfloat16)
 
     def step(n):
-        if n < 16 and n % 4 == 0:
-            for st in streams[1]:
-                st.done(n // 4)
+        if n < 16:
+            need(1, n // 4, n % 4)
         two, three, four = n - 1, n - 3, n - 4
         if 0 <= two < 16:
             pairs(two)
@@ -323,43 +335,68 @@
             keep[block(n)] = partial(n, mine)
             hand(n).start()
 
+    def each(i, call):
+        for st in streams[i]:
+            call(st)
+
+    def last(i):
+        each(i // 16, lambda st: st.last((i // 4) % 4, i % 4))
+
     def on(i):
-        for st in streams[i // 16]:
-            st.last_on((i // 4) % 4, i % 4)
-
-    work = {i: [lambda k=i: norm(k)] for i in range(4)}
-    for r in range(3):
-        work.setdefault(4 * r + 7, []).append(lambda k=r: project(k))
-    work[18] = [lambda: project(3), lambda: keys_values(0), lambda: keys_values(1)]
-    work[19] = [lambda: attend(0, 0), lambda: attend(0, 1)]
-    work[20] = [lambda: attend(1, 0), lambda: attend(1, 1)]
-    for n, o in enumerate((6, 6, 7, 8, 10, 11, 12, 13, 14, 15)):
-        work.setdefault(16 + o, []).append(lambda k=n: step(k))
-
-    for i in range(32):
-        s, r, j = i // 16, (i // 4) % 4, i % 4
-        if i > 0:
-            for st in streams[s]:
-                st.last(r, j)
-        n = i // 4 + 1
-        if n < 8:
-            if j == 0:
-                for st in streams[n // 4]:
-                    st.mid(n % 4)
-            if j == 2:
-                for st in streams[n // 4]:
-                    st.mid_on(n % 4)
-        if i == 8:
-            for st in streams[1]:
-                st.zed()
-        if i == 10:
-            for st in streams[1]:
-                st.zed_on()
-        if i >= LAG:
-            on(i - LAG)
-        for task in work.get(i, ()):
-            task()
-    for i in range(32 - LAG, 32):
+        each(i // 16, lambda st: st.last_on((i // 4) % 4, i % 4))
+
+    def mid(q):
+        each(q // 4, lambda st: st.mid(q % 4))
+
+    def mid_on(q):
+        each(q // 4, lambda st: st.mid_on(q % 4))
+
+    def zed(s):
+        each(s, lambda st: st.zed())
+
+    def zed_on(s):
+        each(s, lambda st: st.zed_on())
+
+    mid(0), last(0), zed(0)
+    fill_gain()
+    load_act.wait()
+    norm(0), norm(1)
+    mid_on(0), last(1), last(2), on(0)
+    norm(2)
+    last(3), on(1), mid(1), zed_on(0)
+    fill_output()
+    norm(3)
+    on(2), last(4), mid_on(1), on(3)
+    last(5), mid(2), last(6), on(4)
+    last(7), mid_on(2), on(5)
+    last(8), mid(3), on(6), zed(1)
+    project(0, (0, 1, 2, 3))
+    last(9), on(7), last(10), mid_on(3), on(8)
+    last(11), zed_on(1), on(9)
+    last(12), mid(4), on(10)
+    project(1, (0, 1, 2, 3))
+    last(13), on(11), last(14), mid_on(4), on(12)
+    last(15), on(13)
+    last(16), mid(5), on(14)
+    project(2, (0, 1, 2, 3))
+    last(17), on(15), last(18), mid_on(5), last(19), last(20)
+    project(3, (0, 1, 2))
+    on(16)
+    project(3, (3,))
+    keys_values(0), keys_values(1)
+    attend(0)
+    last(21), on(17), mid(6)
+    attend(1)
+    step(0)
+    on(18), last(22), mid_on(6), on(19)
+    for n in range(1, 10):
+        step(n)
+        last(n + 22), on(n + 19)
+        if n == 2:
+            mid(7)
+        if n == 4:
+            mid_on(7)
+    for i in range(29, 32):
         on(i)
     for n in range(10, 20):
         step(n)
@@ -375,7 +412,7 @@
             device_id={"tensor": sibling},
             device_id_type=MESH,
         ).wait_send()
-    pltpu.make_async_copy(out, out, io.at[5]).wait()
+    pltpu.make_async_copy(out, out, io.at[1]).wait()
 
 
 def tables():
@@ -389,7 +426,7 @@
     )
 
 
-def layer(activations, gain, qa, qb, oa, ob):
+def layer(activations, gain, *weights):
     vmem = pl.BlockSpec(memory_space=pltpu.VMEM)
     hbm = pl.BlockSpec(memory_space=pltpu.HBM)
     tokens, features = activations.shape
@@ -399,7 +436,7 @@
     return pl.pallas_call(
         layer_kernel,
         out_shape=jax.ShapeDtypeStruct((tokens, features), kind),
-        in_specs=[hbm, vmem, vmem, vmem, hbm, hbm, hbm, hbm],
+        in_specs=[hbm] + [vmem] * 11,
         out_specs=hbm,
         scratch_shapes=[
             pltpu.VMEM((tokens, features), kind),
@@ -418,45 +455,22 @@
             pltpu.VMEM((chunks, SEQ, 256), kind),
             pltpu.VMEM((chunks, SEQ, 256), kind),
             pltpu.VMEM((chunks, tokens, 256), kind),
+            pltpu.VMEM((1, features), jnp.float32),
+            pltpu.VMEM((1024, 64), kind),
             pltpu.SemaphoreType.DMA((2, 2, 64)),
             pltpu.SemaphoreType.DMA((2, 2)),
             pltpu.SemaphoreType.DMA((3, 16)),
             pltpu.SemaphoreType.DMA((3,)),
-            pltpu.SemaphoreType.DMA((6,)),
+            pltpu.SemaphoreType.DMA((2,)),
         ],
         compiler_params=pltpu.CompilerParams(
             collective_id=0, has_side_effects=True, vmem_limit_bytes=60 * 2**20
         ),
-    )(activations, gain, cosine, sine, qa, qb, oa, ob)
-
-
-def dequant(blocks, scales):
-    factor = jnp.exp2(scales.astype(jnp.float32)).astype(blocks.dtype)
-    weight = blocks * factor
-    return weight.reshape(weight.shape[0] * weight.shape[1], weight.shape[2])
-
-
-def shards(
-    activations,
-    norm_gain,
-    query_blocks,
-    query_scales,
-    key_blocks,
-    key_scales,
-    value_blocks,
-    value_scales,
-    output_blocks,
-    output_scales,
-):
-    query = dequant(query_blocks, query_scales)
-    key = dequant(key_blocks, key_scales)
-    value = dequant(value_blocks, value_scales)
-    output = dequant(output_blocks, output_scales).T
-    qa = jnp.concatenate([query[:, :512], key], axis=1)
-    qb = jnp.concatenate([query[:, 512:], value], axis=1)
-    return layer(
-        activations, norm_gain.reshape(1, -1), qa, qb, output[:, :512], output[:, 512:]
-    )
+    )(activations, gain, cosine, sine, *weights)
+
+
+def shards(activations, norm_gain, *weights):
+    return layer(activations, norm_gain.reshape(32, 128), *weights)
 
 
 def solution(mesh):

time: 175 us -> 140 us (0.80)
  Pallas kernels: 160 us -> 135 us
  other arithmetic: 6.84 us -> 0 us
  local copies, waits for them, and re-layouts: 6.81 us -> 4.7 us
    pallas_call x1, Pallas kernels: 160 us -> 135 us  [layer(): pl.pallas_call(layer_kernel, out_shape=jax.ShapeDtypeStruct((tokens, feat...]
    mul x4 -> x0, other arithmetic: 3.34 us -> none  [dequant(): weight = blocks * factor]
    convert_element_type x4 -> x0, other arithmetic: 2.84 us -> none  [dequant(): factor = jnp.exp2(scales.astype(jnp.float32)).astype(blocks.dtype)]
    unnamed x5 -> x1, local copies, waits for them, and re-layouts: 4.72 us -> 4.7 us
where the time goes in v3:
time: 140 us
  Pallas kernels  135 us (96%)
  local copies, waits for them, and re-layouts  4.7 us (3%)
    pallas_call x1, Pallas kernels, layer(): pl.pallas_call(layer_kernel, out_shape=jax.ShapeDtypeStruct((tokens, feat...  135 us
    unnamed x1, local copies, waits for them, and re-layouts  4.7 us

profile of v3, /device:TPU:1, one launch (start us, length us, event | category | flops | bytes accessed | tf_op | source)
XLA Modules:
  0.0 140.2 jit_solution(4817412190521858278)
XLA Ops:
  0.0 135.5 %shard_map.118 = bf16[512,4096]{1,0:T(8,128)(2,1)} custom-call(bf16[512,4096]{1,0:T(8,128)(2,1)} %act_in.1, bf16[32,128]{1,0:T(8,128)(2,1)} %bitcast.1, f32[256,128]{1,0:T(8,128)} %constant.4.clone.cosine, f32[256,128]{1,0:T(8,128)} %constant.5.clone.sine, bf16[2,32,1024]{2,1,0:T(8,128)(2,1)} %query_in.1, s32[2,1,1024]{2,1,0:T(1,128)} %query_exp.1, ...), custom_call_target="tpu_custom_call" | custom-call | tf_op jit(solution)/shard_map/pallas_call | solution.py:436
  135.5 4.7 %copy.14 = bf16[512,4096]{1,0:T(8,128)(2,1)} copy(bf16[512,4096]{1,0:T(8,128)(2,1)} %shard_map.118) | data formatting | bytes 8388608

commit v4 on v3

--- a/solution.py
+++ b/solution.py
@@ -22,8 +22,9 @@
 
 
 class Half:
-    def __init__(self, half, buf, recv, send, place):
+    def __init__(self, half, buf, recv, send, place, spins, toward):
         self.half, self.buf, self.recv, self.sent = half, buf, recv, send
+        self.spins, self.toward = spins, toward
         x, y, z = place
         self.z = z
         self.m, self.l = (x, y) if half == 0 else (y, x)
@@ -34,7 +35,7 @@
 
     def slot(self, key):
         r, jm, jl = key
-        return self.index(turn(self.m, OFF[jm]), turn(self.l, OFF[jl]), turn(self.z, OFF[r]))
+        return self.index(turn(self.m, OFF[jm]), turn(self.l, OFF[jl]), turn(self.z, self.spins[r]))
 
     def rows(self, key):
         return self.buf.at[pl.ds(pl.multiple_of(self.slot(key) * ROWS, ROWS), ROWS)]
@@ -77,11 +78,12 @@
             self.ensure(key_plus)
             self.copy(key_plus, self.near(dim, -1)).start()
 
-    def zed(self):
+    def start(self):
         self.both((0, 0, 0), "z")
 
-    def zed_on(self):
-        self.forward((1, 0, 0), (2, 0, 0), "z", self.half)
+    def start_on(self):
+        self.ensure((1, 0, 0))
+        self.copy((1, 0, 0), self.near("z", self.toward)).start()
 
     def mid(self, r):
         self.both((r, 0, 0), "m")
@@ -129,6 +131,7 @@
     output_in,
     output_exp,
     out,
+    raw,
     act,
     qa,
     qb,
@@ -151,23 +154,48 @@
     sent,
     sum_recv,
     sum_sent,
+    swap_recv,
+    swap_sent,
     io,
 ):
     dp = lax.axis_index("dp")
     tensor = lax.axis_index("tensor")
     x, z, y = lax.rem(dp, 4), lax.rem(dp // 4, 4), dp // 16
     core = lax.rem(tensor, 2)
-    sibling = tensor + 1 - 2 * core
-    partner = lax.rem(tensor + 2, 4)
+    side = tensor // 2
+    sibling = {"tensor": tensor + 1 - 2 * core}
+    twin = {"tensor": lax.rem(tensor + 2, 4)}
+    peer = {
+        "dp": y * 16 + lax.rem(z + 3 - 2 * side, 4) * 4 + x,
+        "tensor": lax.rem(tensor + 2, 4),
+    }
     mine = pl.ds(pl.multiple_of(core * SEQ, SEQ), SEQ)
     other = pl.ds(pl.multiple_of((1 - core) * SEQ, SEQ), SEQ)
+
+    def quarter(sequence, half):
+        return pl.ds(pl.multiple_of(sequence * SEQ + half * 128, 128), 128)
+
     bufs = ((qa, qb), (oa, ob))
+    spins = ((0, -1, 1, 2), (0, 3 + 2 * side, 1 + side, 2 + side))
+    twin_spins = (0, 5 - 2 * side, 2 - side, 3 - side)
     streams = [
-        [Half(h, bufs[s][h], recv.at[s, h], sent.at[s, h], (x, y, z)) for h in range(2)]
-        for s in range(2)
+        [
+            Half(
+                h,
+                bufs[k][h],
+                recv.at[k, h],
+                sent.at[k, h],
+                (x, y, z),
+                spins[k],
+                (1, 1 + 2 * side)[k],
+            )
+            for h in range(2)
+        ]
+        for k in range(2)
     ]
     first = streams[0][0]
-    load_act = pltpu.make_async_copy(act_in, act, io.at[0])
+    kept = pl.ds(pl.multiple_of(side * SEQ, SEQ), SEQ)
+    load_act = pltpu.make_async_copy(act_in.at[kept], raw.at[:SEQ], io.at[0])
     load_act.start()
     barrier = pltpu.get_barrier_semaphore()
     for dim in ("m", "l", "z"):
@@ -175,8 +203,8 @@
             pl.semaphore_signal(
                 barrier, inc=1, device_id={"dp": first.near(dim, d)}, device_id_type=MESH
             )
-    for peer in (sibling, partner):
-        pl.semaphore_signal(barrier, inc=1, device_id={"tensor": peer}, device_id_type=MESH)
+    for device in (sibling, twin, peer):
+        pl.semaphore_signal(barrier, inc=1, device_id=device, device_id_type=MESH)
 
     def factor(exponents):
         return jnp.exp2(exponents.astype(jnp.float32)).astype(jnp.bfloat16)
@@ -202,13 +230,37 @@
         acc_a[...] = jnp.zeros_like(acc_a)
         acc_b[...] = jnp.zeros_like(acc_b)
 
-    pl.semaphore_wait(barrier, 8)
+    fill_output()
+    pl.semaphore_wait(barrier, 9)
+
+    def swap_copy(stage, p, source, half, device):
+        piece = pl.ds(pl.multiple_of(source * SEQ + half * 128 + p * 32, 32), 32)
+        there = pl.ds(pl.multiple_of(SEQ + half * 128 + p * 32, 32), 32)
+        return pltpu.make_async_remote_copy(
+            src_ref=raw.at[piece],
+            dst_ref=raw.at[there],
+            send_sem=swap_sent.at[stage],
+            recv_sem=swap_recv.at[stage, p],
+            device_id=device,
+            device_id_type=MESH,
+        )
+
+    def swap(p):
+        swap_copy(0, p, 0, core, peer).start()
+
+    def swap_on(p):
+        swap_copy(0, p, 0, core, peer).wait_recv()
+        swap_copy(1, p, 1, core, sibling).start()
+
+    def swap_done():
+        for p in range(4):
+            swap_copy(1, p, 1, 1 - core, sibling).wait_recv()
 
     def norm(k):
         @pl.loop(0, 8)
         def _(i):
             rows = pl.ds(pl.multiple_of(k * 128 + i * 16, 16), 16)
-            wide = act[rows, :].astype(jnp.float32)
+            wide = raw[rows, :].astype(jnp.float32)
             mean = jnp.mean(wide * wide, axis=-1, keepdims=True)
             scaled = wide * lax.rsqrt(mean + EPS) * gain_row[...]
             act[rows, :] = scaled.astype(jnp.bfloat16)
@@ -240,59 +292,55 @@
         keys[rows, :] = rotate(acc_a[rows, 512:]).astype(jnp.bfloat16)
         values[rows, :] = acc_b[rows, 512:].astype(jnp.bfloat16)
 
-    def attend(h):
+    def attend(h, s):
         acc = (acc_a, acc_b)[h]
-
-        @pl.loop(0, 2)
-        def _(s):
-            rows = pl.ds(pl.multiple_of(s * SEQ, SEQ), SEQ)
-            spot = lax.broadcasted_iota(jnp.int32, (SEQ, SEQ), 0)
-            seen = lax.broadcasted_iota(jnp.int32, (SEQ, SEQ), 1)
-            for k in range(4):
-                queries = rotate(acc[rows, k * HEAD_DIM : (k + 1) * HEAD_DIM])
-                scores = product_t(queries.astype(jnp.bfloat16), keys[rows, :])
-                scores = scores * HEAD_DIM ** (-0.5)
-                scores = jnp.where(spot >= seen, scores, -jnp.inf)
-                raised = jnp.exp(scores - jnp.max(scores, axis=-1, keepdims=True))
-                weights = raised * (1.0 / jnp.sum(raised, axis=-1, keepdims=True))
-                wide = product(weights.astype(jnp.bfloat16), values[rows, :])
-                place = h * 512 + k * HEAD_DIM
-                context[rows, place : place + HEAD_DIM] = wide.astype(jnp.bfloat16)
-
-    def block(n):
-        return turn(y, OFF[n % 4]) * 4 + turn(z, OFF[n // 4])
-
-    def tensor_copy(stage, n, src, dst, peer):
-        c = block(n)
+        rows = pl.ds(s * SEQ, SEQ)
+        spot = lax.broadcasted_iota(jnp.int32, (SEQ, SEQ), 0)
+        seen = lax.broadcasted_iota(jnp.int32, (SEQ, SEQ), 1)
+        for k in range(4):
+            queries = rotate(acc[rows, k * HEAD_DIM : (k + 1) * HEAD_DIM])
+            scores = product_t(queries.astype(jnp.bfloat16), keys[rows, :])
+            scores = scores * HEAD_DIM ** (-0.5)
+            scores = jnp.where(spot >= seen, scores, -jnp.inf)
+            raised = jnp.exp(scores - jnp.max(scores, axis=-1, keepdims=True))
+            weights = raised * (1.0 / jnp.sum(raised, axis=-1, keepdims=True))
+            wide = product(weights.astype(jnp.bfloat16), values[rows, :]).astype(jnp.bfloat16)
+            place = slice(h * 512 + k * HEAD_DIM, h * 512 + (k + 1) * HEAD_DIM)
+            context[s * 128 : s * 128 + 128, place] = wide[:128]
+            context[SEQ + s * 128 : SEQ + s * 128 + 128, place] = wide[128:]
+
+    def block(n, turns=spins[1]):
+        return turn(y, OFF[n % 4]) * 4 + turn(z, turns[n // 4])
+
+    def twin_block(n):
+        return block(n, twin_spins)
+
+    def sum_copy(stage, c, src, dst, device):
         return pltpu.make_async_remote_copy(
             src_ref=src,
             dst_ref=dst,
             send_sem=sum_sent.at[stage],
             recv_sem=sum_recv.at[stage, c],
-            device_id={"tensor": peer},
+            device_id=device,
             device_id_type=MESH,
         )
 
     def hand(n):
         c = block(n)
-        return tensor_copy(0, n, give.at[c], got.at[c], sibling)
+        return sum_copy(0, c, give.at[c], got.at[c], sibling)
 
     def cross(n):
         c = block(n)
-        return tensor_copy(1, n, pair.at[c], over.at[c], partner)
-
-    def share(n):
-        c = block(n)
-        return tensor_copy(2, n, total.at[c, mine], total.at[c, mine], sibling)
-
-    def share_in(n):
-        c = block(n)
-        return tensor_copy(2, n, total.at[c, other], total.at[c, other], sibling)
-
-    def put(n, half):
-        c = block(n)
+        return sum_copy(1, c, pair.at[c, 128:], over.at[c], peer)
+
+    def spread(stage, c, sequence, half, device):
+        piece = total.at[c, quarter(sequence, half)]
+        return sum_copy(stage, c, piece, piece, device)
+
+    def put(c, sequence):
+        rows = pl.ds(pl.multiple_of(sequence * SEQ, SEQ), SEQ)
         columns = pl.ds(pl.multiple_of(c * 256, 256), 256)
-        return pltpu.make_async_copy(total.at[c, half], out.at[half, columns], io.at[1])
+        return pltpu.make_async_copy(total.at[c, rows], out.at[rows, columns], io.at[1])
 
     def partial(n, rows):
         part = pl.ds(pl.multiple_of(block(n) * 256, 256), 256)
@@ -310,30 +358,43 @@
     def totals(n):
         c = block(n)
         cross(n).wait_recv()
-        wide = pair[c].astype(jnp.float32) + over[c].astype(jnp.float32)
-        total[c, mine, :] = wide.astype(jnp.bfloat16)
+        wide = pair[c, :128, :].astype(jnp.float32) + over[c].astype(jnp.float32)
+        total[c, quarter(side, core), :] = wide.astype(jnp.bfloat16)
+
+    def due(n):
+        return tuple(m for m in range(16) if n == (m + 9 if m < 4 else m + 4))
+
+    def tell(m):
+        spread(3, block(m), side, core, twin).start()
+        spread(2, block(m), side, core, sibling).start()
+
+    def relay(m):
+        spread(3, twin_block(m), 1 - side, core, twin).wait_recv()
+        spread(4, twin_block(m), 1 - side, core, sibling).start()
+
+    def finish(m):
+        spread(2, block(m), side, 1 - core, sibling).wait_recv()
+        put(block(m), side).start()
+        spread(4, twin_block(m), 1 - side, 1 - core, sibling).wait_recv()
+        put(twin_block(m), 1 - side).start()
 
     def step(n):
-        if n < 16:
-            need(1, n // 4, n % 4)
-        two, three, four = n - 1, n - 3, n - 4
-        if 0 <= two < 16:
-            pairs(two)
-        if 0 <= three < 16:
-            totals(three)
-        if n < 16:
-            give[block(n)] = partial(n, other)
-        if 0 <= two < 16:
-            cross(two).start()
-        if 0 <= three < 16:
-            share(three).start()
-            put(three, mine).start()
-        if 0 <= four < 16:
-            share_in(four).wait_recv()
-            put(four, other).start()
-        if n < 16:
-            keep[block(n)] = partial(n, mine)
-            hand(n).start()
+        need(1, n // 4, n % 4)
+        if n >= 2:
+            pairs(n - 2)
+        for m in due(n):
+            totals(m)
+        give[block(n)] = partial(n, other)
+        if n >= 2:
+            cross(n - 2).start()
+        for m in due(n):
+            tell(m)
+        for m in due(n - 4):
+            relay(m)
+        for m in due(n - 6):
+            finish(m)
+        keep[block(n)] = partial(n, mine)
+        hand(n).start()
 
     def each(i, call):
         for st in streams[i]:
@@ -351,65 +412,91 @@
     def mid_on(q):
         each(q // 4, lambda st: st.mid_on(q % 4))
 
-    def zed(s):
-        each(s, lambda st: st.zed())
-
-    def zed_on(s):
-        each(s, lambda st: st.zed_on())
-
-    mid(0), last(0), zed(0)
+    def start(s):
+        each(s, lambda st: st.start())
+
+    def start_on(s):
+        each(s, lambda st: st.start_on())
+
+    whole = (0, 1, 2, 3)
+    mid(0), last(0), start(0), mid(4), last(16)
     fill_gain()
     load_act.wait()
+    swap(0), swap(1)
     norm(0), norm(1)
     mid_on(0), last(1), last(2), on(0)
-    norm(2)
-    last(3), on(1), mid(1), zed_on(0)
-    fill_output()
-    norm(3)
+    last(3), on(1), mid(1), start_on(0)
+    swap(2), swap(3)
     on(2), last(4), mid_on(1), on(3)
     last(5), mid(2), last(6), on(4)
+    swap_on(0)
     last(7), mid_on(2), on(5)
-    last(8), mid(3), on(6), zed(1)
-    project(0, (0, 1, 2, 3))
+    last(8), mid(3), on(6)
+    swap_on(1)
     last(9), on(7), last(10), mid_on(3), on(8)
-    last(11), zed_on(1), on(9)
-    last(12), mid(4), on(10)
-    project(1, (0, 1, 2, 3))
-    last(13), on(11), last(14), mid_on(4), on(12)
+    swap_on(2)
+    last(11), on(9), start(1)
+    last(12), on(10)
+    swap_on(3)
+    last(13), on(11), last(14)
+    swap_done()
+    norm(2), norm(3)
+    mid_on(4), on(12)
+    project(0, whole)
     last(15), on(13)
-    last(16), mid(5), on(14)
-    project(2, (0, 1, 2, 3))
-    last(17), on(15), last(18), mid_on(5), last(19), last(20)
+    project(1, whole)
+    on(14), start_on(1)
+    project(2, whole)
+    last(17), on(15), last(18), last(19)
     project(3, (0, 1, 2))
-    on(16)
+    on(16), mid(5)
     project(3, (3,))
     keys_values(0), keys_values(1)
-    attend(0)
-    last(21), on(17), mid(6)
-    attend(1)
-    step(0)
-    on(18), last(22), mid_on(6), on(19)
-    for n in range(1, 10):
+    attend(0, 0)
+    on(17), last(20)
+    attend(0, 1)
+    on(18), mid_on(5)
+    attend(1, 0)
+    on(19), last(21)
+    attend(1, 1)
+    step(0), last(22), mid(6), on(20)
+    step(1), last(23), on(21)
+    step(2), last(24), mid_on(6), on(22)
+    step(3), last(25), mid(7), on(23)
+    step(4), last(26), on(24)
+    step(5), last(27), mid_on(7), on(25)
+    step(6), last(28), on(26)
+    step(7), last(29), on(27)
+    step(8), last(30), on(28)
+    step(9), last(31), on(29)
+    step(10), on(30)
+    step(11), on(31)
+    for n in range(12, 16):
         step(n)
-        last(n + 22), on(n + 19)
-        if n == 2:
-            mid(7)
-        if n == 4:
-            mid_on(7)
-    for i in range(29, 32):
-        on(i)
-    for n in range(10, 20):
-        step(n)
+    pairs(14), pairs(15)
+    cross(14).start(), relay(3), cross(15).start()
+    totals(12), relay(8), tell(12)
+    totals(13), relay(9), tell(13)
+    totals(14), relay(10), tell(14)
+    totals(15), relay(11), tell(15)
+    for m in (1, 2, 3, 6, 7, 8, 9, 10):
+        finish(m)
+    relay(12), finish(11), relay(13), finish(12), relay(14), finish(13), relay(15)
+    finish(14), finish(15)
     for s in range(2):
         for st in streams[s]:
             st.drain()
-    for stage, ref in enumerate((give, pair, total.at[:, :SEQ])):
+    part = total.at[:, :128]
+    for stage, ref in enumerate((give, pair.at[:, 128:], part, part, part)):
+        sum_copy(stage, 0, ref, ref, sibling).wait_send()
+    part = raw.at[:128]
+    for stage in range(2):
         pltpu.make_async_remote_copy(
-            src_ref=ref,
-            dst_ref=ref,
-            send_sem=sum_sent.at[stage],
-            recv_sem=sum_recv.at[stage, 0],
-            device_id={"tensor": sibling},
+            src_ref=part,
+            dst_ref=part,
+            send_sem=swap_sent.at[stage],
+            recv_sem=swap_recv.at[stage, 0],
+            device_id=sibling,
             device_id_type=MESH,
         ).wait_send()
     pltpu.make_async_copy(out, out, io.at[1]).wait()
@@ -440,6 +527,7 @@
         out_specs=hbm,
         scratch_shapes=[
             pltpu.VMEM((tokens, features), kind),
+            pltpu.VMEM((tokens, features), kind),
             pltpu.VMEM((features, 640), kind),
             pltpu.VMEM((features, 640), kind),
             pltpu.VMEM((features, 512), kind),
@@ -453,14 +541,16 @@
             pltpu.VMEM((chunks, SEQ, 256), kind),
             pltpu.VMEM((chunks, SEQ, 256), kind),
             pltpu.VMEM((chunks, SEQ, 256), kind),
-            pltpu.VMEM((chunks, SEQ, 256), kind),
+            pltpu.VMEM((chunks, 128, 256), kind),
             pltpu.VMEM((chunks, tokens, 256), kind),
             pltpu.VMEM((1, features), jnp.float32),
             pltpu.VMEM((1024, 64), kind),
             pltpu.SemaphoreType.DMA((2, 2, 64)),
             pltpu.SemaphoreType.DMA((2, 2)),
-            pltpu.SemaphoreType.DMA((3, 16)),
-            pltpu.SemaphoreType.DMA((3,)),
+            pltpu.SemaphoreType.DMA((5, 16)),
+            pltpu.SemaphoreType.DMA((5,)),
+            pltpu.SemaphoreType.DMA((2, 4)),
+            pltpu.SemaphoreType.DMA((2,)),
             pltpu.SemaphoreType.DMA((2,)),
         ],
         compiler_params=pltpu.CompilerParams(

time: 140 us -> 133 us (0.950)
  Pallas kernels: 135 us -> 128 us
    pallas_call x1, Pallas kernels: 135 us -> 128 us  [layer(): pl.pallas_call(layer_kernel, out_shape=jax.ShapeDtypeStruct((tokens, feat...]
where the time goes in v4:
time: 133 us
  Pallas kernels  128 us (96%)
  local copies, waits for them, and re-layouts  4.7 us (4%)
    pallas_call x1, Pallas kernels, layer(): pl.pallas_call(layer_kernel, out_shape=jax.ShapeDtypeStruct((tokens, feat...  128 us
    unnamed x1, local copies, waits for them, and re-layouts  4.7 us

profile of v4, /device:TPU:1, one launch (start us, length us, event | category | flops | bytes accessed | tf_op | source)
XLA Modules:
  0.0 133.1 jit_solution(16704081287853131121)
XLA Ops:
  0.0 128.4 %shard_map.118 = bf16[512,4096]{1,0:T(8,128)(2,1)} custom-call(bf16[512,4096]{1,0:T(8,128)(2,1)} %act_in.1, bf16[32,128]{1,0:T(8,128)(2,1)} %bitcast.1, f32[256,128]{1,0:T(8,128)} %constant.4.clone.cosine, f32[256,128]{1,0:T(8,128)} %constant.5.clone.sine, bf16[2,32,1024]{2,1,0:T(8,128)(2,1)} %query_in.1, s32[2,1,1024]{2,1,0:T(1,128)} %query_exp.1, ...), custom_call_target="tpu_custom_call" | custom-call | tf_op jit(solution)/shard_map/pallas_call | solution.py:523
  128.4 4.7 %copy.14 = bf16[512,4096]{1,0:T(8,128)(2,1)} copy(bf16[512,4096]{1,0:T(8,128)(2,1)} %shard_map.118) | data formatting | bytes 8388608

commit v5 on v4

--- a/solution.py
+++ b/solution.py
@@ -119,17 +119,17 @@
 
 def layer_kernel(
     act_in,
-    gain,
-    cosine,
-    sine,
-    query_in,
-    query_exp,
-    key_in,
-    key_exp,
-    value_in,
-    value_exp,
-    output_in,
-    output_exp,
+    gain_hbm,
+    cosine_hbm,
+    sine_hbm,
+    query_in_hbm,
+    query_exp_hbm,
+    key_in_hbm,
+    key_exp_hbm,
+    value_in_hbm,
+    value_exp_hbm,
+    output_in_hbm,
+    output_exp_hbm,
     out,
     raw,
     act,
@@ -150,6 +150,17 @@
     total,
     gain_row,
     flat,
+    gain,
+    cosine,
+    sine,
+    query_in,
+    query_exp,
+    key_in,
+    key_exp,
+    value_in,
+    value_exp,
+    output_in,
+    output_exp,
     recv,
     sent,
     sum_recv,
@@ -196,6 +207,26 @@
     first = streams[0][0]
     kept = pl.ds(pl.multiple_of(side * SEQ, SEQ), SEQ)
     load_act = pltpu.make_async_copy(act_in.at[kept], raw.at[:SEQ], io.at[0])
+    loads = [
+        pltpu.make_async_copy(src, dst, io.at[k + 2])
+        for k, (src, dst) in enumerate(
+            (
+                (query_in_hbm, query_in),
+                (query_exp_hbm, query_exp),
+                (key_in_hbm, key_in),
+                (key_exp_hbm, key_exp),
+                (value_in_hbm, value_in),
+                (value_exp_hbm, value_exp),
+                (output_in_hbm, output_in),
+                (output_exp_hbm, output_exp),
+                (gain_hbm, gain),
+                (cosine_hbm, cosine),
+                (sine_hbm, sine),
+            )
+        )
+    ]
+    for load in loads:
+        load.start()
     load_act.start()
     barrier = pltpu.get_barrier_semaphore()
     for dim in ("m", "l", "z"):
@@ -209,6 +240,8 @@
     def factor(exponents):
         return jnp.exp2(exponents.astype(jnp.float32)).astype(jnp.bfloat16)
 
+    for load in loads:
+        load.wait()
     for b in range(2):
         rows = pl.ds(pl.multiple_of(dp * ROWS + b * 32, 32), 32)
         query = query_in[b] * factor(query_exp[b])
@@ -362,7 +395,7 @@
         total[c, quarter(side, core), :] = wide.astype(jnp.bfloat16)
 
     def due(n):
-        return tuple(m for m in range(16) if n == (m + 9 if m < 4 else m + 4))
+        return tuple(m for m in range(16) if n == m + (8, 3, 5, 5)[m // 4])
 
     def tell(m):
         spread(3, block(m), side, core, twin).start()
@@ -382,19 +415,19 @@
         need(1, n // 4, n % 4)
         if n >= 2:
             pairs(n - 2)
+        give[block(n)] = partial(n, other)
+        keep[block(n)] = partial(n, mine)
+        if n >= 2:
+            cross(n - 2).start()
+        hand(n).start()
         for m in due(n):
             totals(m)
-        give[block(n)] = partial(n, other)
-        if n >= 2:
-            cross(n - 2).start()
-        for m in due(n):
-            tell(m)
         for m in due(n - 4):
             relay(m)
         for m in due(n - 6):
             finish(m)
-        keep[block(n)] = partial(n, mine)
-        hand(n).start()
+        for m in due(n):
+            tell(m)
 
     def each(i, call):
         for st in streams[i]:
@@ -473,16 +506,16 @@
     step(11), on(31)
     for n in range(12, 16):
         step(n)
-    pairs(14), pairs(15)
-    cross(14).start(), relay(3), cross(15).start()
-    totals(12), relay(8), tell(12)
-    totals(13), relay(9), tell(13)
-    totals(14), relay(10), tell(14)
-    totals(15), relay(11), tell(15)
-    for m in (1, 2, 3, 6, 7, 8, 9, 10):
-        finish(m)
-    relay(12), finish(11), relay(13), finish(12), relay(14), finish(13), relay(15)
-    finish(14), finish(15)
+    pairs(14), finish(2), finish(3), finish(7)
+    cross(14).start()
+    pairs(15), totals(11)
+    cross(15).start(), relay(8), tell(11)
+    totals(12), relay(9), tell(12)
+    totals(13), finish(8), tell(13)
+    totals(14), finish(9), tell(14)
+    totals(15), relay(10), tell(15)
+    relay(11), finish(10), relay(12), finish(11), relay(13), finish(12), relay(14)
+    finish(13), relay(15), finish(14), finish(15)
     for s in range(2):
         for st in streams[s]:
             st.drain()
@@ -520,10 +553,11 @@
     cosine, sine = tables()
     kind = jnp.bfloat16
     chunks = features // 256
+    small = (gain, cosine, sine, *weights)
     return pl.pallas_call(
         layer_kernel,
         out_shape=jax.ShapeDtypeStruct((tokens, features), kind),
-        in_specs=[hbm] + [vmem] * 11,
+        in_specs=[hbm] * 12,
         out_specs=hbm,
         scratch_shapes=[
             pltpu.VMEM((tokens, features), kind),
@@ -545,18 +579,19 @@
             pltpu.VMEM((chunks, tokens, 256), kind),
             pltpu.VMEM((1, features), jnp.float32),
             pltpu.VMEM((1024, 64), kind),
+            *(pltpu.VMEM(a.shape, a.dtype) for a in small),
             pltpu.SemaphoreType.DMA((2, 2, 64)),
             pltpu.SemaphoreType.DMA((2, 2)),
             pltpu.SemaphoreType.DMA((5, 16)),
             pltpu.SemaphoreType.DMA((5,)),
             pltpu.SemaphoreType.DMA((2, 4)),
             pltpu.SemaphoreType.DMA((2,)),
-            pltpu.SemaphoreType.DMA((2,)),
+            pltpu.SemaphoreType.DMA((13,)),
         ],
         compiler_params=pltpu.CompilerParams(
             collective_id=0, has_side_effects=True, vmem_limit_bytes=60 * 2**20
         ),
-    )(activations, gain, cosine, sine, *weights)
+    )(activations, *small)
 
 
 def shards(activations, norm_gain, *weights):

time: 133 us -> 130 us (0.977)
  Pallas kernels: 128 us -> 125 us
    pallas_call x1, Pallas kernels: 128 us -> 125 us  [layer(): pl.pallas_call(layer_kernel, out_shape=jax.ShapeDtypeStruct((tokens, feat...]
where the time goes in v5:
time: 130 us
  Pallas kernels  125 us (96%)
  local copies, waits for them, and re-layouts  4.7 us (4%)
    pallas_call x1, Pallas kernels, layer(): pl.pallas_call(layer_kernel, out_shape=jax.ShapeDtypeStruct((tokens, feat...  125 us
    unnamed x1, local copies, waits for them, and re-layouts  4.7 us

profile of v5, /device:TPU:1, one launch (start us, length us, event | category | flops | bytes accessed | tf_op | source)
XLA Modules:
  0.0 130.1 jit_solution(2644563934829018525)
XLA Ops:
  0.0 125.4 %shard_map.118 = bf16[512,4096]{1,0:T(8,128)(2,1)} custom-call(bf16[512,4096]{1,0:T(8,128)(2,1)} %act_in.1, bf16[32,128]{1,0:T(8,128)(2,1)} %bitcast.1, f32[256,128]{1,0:T(8,128)} %constant.4.clone.cosine_hbm, f32[256,128]{1,0:T(8,128)} %constant.5.clone.sine_hbm, bf16[2,32,1024]{2,1,0:T(8,128)(2,1)} %query_in_hbm.1, s32[2,1,1024]{2,1,0:T(1,128)} %query_exp_hbm.1, ...), custom_call_target="tpu_custom_call" | custom-call | tf_op jit(solution)/shard_map/pallas_call | solution.py:557
  125.4 4.7 %copy.14 = bf16[512,4096]{1,0:T(8,128)(2,1)} copy(bf16[512,4096]{1,0:T(8,128)(2,1)} %shard_map.118) | data formatting | bytes 8388608

commit v6 on v5

--- a/solution.py
+++ b/solution.py
@@ -130,7 +130,7 @@
     value_exp_hbm,
     output_in_hbm,
     output_exp_hbm,
-    out,
+    total,
     raw,
     act,
     qa,
@@ -147,7 +147,6 @@
     got,
     pair,
     over,
-    total,
     gain_row,
     flat,
     gain,
@@ -370,11 +369,6 @@
         piece = total.at[c, quarter(sequence, half)]
         return sum_copy(stage, c, piece, piece, device)
 
-    def put(c, sequence):
-        rows = pl.ds(pl.multiple_of(sequence * SEQ, SEQ), SEQ)
-        columns = pl.ds(pl.multiple_of(c * 256, 256), 256)
-        return pltpu.make_async_copy(total.at[c, rows], out.at[rows, columns], io.at[1])
-
     def partial(n, rows):
         part = pl.ds(pl.multiple_of(block(n) * 256, 256), 256)
         wide = product_t(context[rows, :512], oa[part, :]) + product_t(
@@ -407,9 +401,7 @@
 
     def finish(m):
         spread(2, block(m), side, 1 - core, sibling).wait_recv()
-        put(block(m), side).start()
         spread(4, twin_block(m), 1 - side, 1 - core, sibling).wait_recv()
-        put(twin_block(m), 1 - side).start()
 
     def step(n):
         need(1, n // 4, n % 4)
@@ -506,14 +498,14 @@
     step(11), on(31)
     for n in range(12, 16):
         step(n)
-    pairs(14), finish(2), finish(3), finish(7)
-    cross(14).start()
-    pairs(15), totals(11)
-    cross(15).start(), relay(8), tell(11)
-    totals(12), relay(9), tell(12)
-    totals(13), finish(8), tell(13)
-    totals(14), finish(9), tell(14)
-    totals(15), relay(10), tell(15)
+    pairs(14), pairs(15)
+    cross(14).start(), totals(11)
+    cross(15).start(), finish(2), tell(11)
+    totals(12), relay(8), tell(12)
+    totals(13), relay(9), tell(13)
+    totals(14), finish(3), tell(14)
+    totals(15), finish(7), tell(15)
+    relay(10), finish(8), finish(9)
     relay(11), finish(10), relay(12), finish(11), relay(13), finish(12), relay(14)
     finish(13), relay(15), finish(14), finish(15)
     for s in range(2):
@@ -532,7 +524,6 @@
             device_id=sibling,
             device_id_type=MESH,
         ).wait_send()
-    pltpu.make_async_copy(out, out, io.at[1]).wait()
 
 
 def tables():
@@ -553,12 +544,15 @@
     cosine, sine = tables()
     kind = jnp.bfloat16
     chunks = features // 256
-    small = (gain, cosine, sine, *weights)
+    small = [
+        pltpu.with_memory_space_constraint(jnp.asarray(a), pltpu.HBM)
+        for a in (gain, cosine, sine, *weights)
+    ]
     return pl.pallas_call(
         layer_kernel,
-        out_shape=jax.ShapeDtypeStruct((tokens, features), kind),
+        out_shape=jax.ShapeDtypeStruct((chunks, tokens, 256), kind),
         in_specs=[hbm] * 12,
-        out_specs=hbm,
+        out_specs=vmem,
         scratch_shapes=[
             pltpu.VMEM((tokens, features), kind),
             pltpu.VMEM((tokens, features), kind),
@@ -576,7 +570,6 @@
             pltpu.VMEM((chunks, SEQ, 256), kind),
             pltpu.VMEM((chunks, SEQ, 256), kind),
             pltpu.VMEM((chunks, 128, 256), kind),
-            pltpu.VMEM((chunks, tokens, 256), kind),
             pltpu.VMEM((1, features), jnp.float32),
             pltpu.VMEM((1024, 64), kind),
             *(pltpu.VMEM(a.shape, a.dtype) for a in small),
@@ -589,13 +582,32 @@
             pltpu.SemaphoreType.DMA((13,)),
         ],
         compiler_params=pltpu.CompilerParams(
-            collective_id=0, has_side_effects=True, vmem_limit_bytes=60 * 2**20
+            collective_id=0, has_side_effects=True, vmem_limit_bytes=48 * 2**20
         ),
     )(activations, *small)
 
 
+def place_kernel(blocks, out, sent):
+    copies = [
+        pltpu.make_async_copy(blocks.at[c], out.at[:, pl.ds(c * 256, 256)], sent.at[c])
+        for c in range(blocks.shape[0])
+    ]
+    for copy in copies:
+        copy.start()
+    for copy in copies:
+        copy.wait()
+
+
 def shards(activations, norm_gain, *weights):
-    return layer(activations, norm_gain.reshape(32, 128), *weights)
+    blocks = layer(activations, norm_gain.reshape(32, 128), *weights)
+    return pl.pallas_call(
+        place_kernel,
+        out_shape=jax.ShapeDtypeStruct(activations.shape, activations.dtype),
+        in_specs=[pl.BlockSpec(memory_space=pltpu.VMEM)],
+        out_specs=pl.BlockSpec(memory_space=pltpu.HBM),
+        scratch_shapes=[pltpu.SemaphoreType.DMA((blocks.shape[0],))],
+        compiler_params=pltpu.CompilerParams(vmem_limit_bytes=2**20),
+    )(blocks)
 
 
 def solution(mesh):

time: 130 us -> 127 us (0.977)
  local copies, waits for them, and re-layouts: 4.7 us -> 0 us
  Pallas kernels: 125 us -> 127 us
    unnamed x1 -> x0, local copies, waits for them, and re-layouts: 4.7 us -> none
    pallas_call x1 -> x2, Pallas kernels: 125 us -> 127 us  [the longest x1 125 us: layer(): pl.pallas_call(layer_kernel, out_shape=jax.ShapeDtypeStruct((chunks, toke...]
where the time goes in v6:
time: 127 us
  Pallas kernels  127 us (100%)
    pallas_call x1, Pallas kernels, layer(): pl.pallas_call(layer_kernel, out_shape=jax.ShapeDtypeStruct((chunks, toke...  125 us

profile of v6, /device:TPU:1, one launch (start us, length us, event | category | flops | bytes accessed | tf_op | source)
XLA Modules:
  0.0 127.1 jit_solution(8625055159248575426)
XLA Ops:
  0.0 124.8 %shard_map.118.blocks = bf16[16,512,256]{2,1,0:T(8,128)(2,1)S(1)} custom-call(bf16[512,4096]{1,0:T(8,128)(2,1)} %act_in.1, bf16[32,128]{1,0:T(8,128)(2,1)} %bitcast.1, f32[256,128]{1,0:T(8,128)} %constant.4.clone.cosine_hbm, f32[256,128]{1,0:T(8,128)} %constant.5.clone.sine_hbm, bf16[2,32,1024]{2,1,0:T(8,128)(2,1)} %query_in_hbm.1, ...), custom_call_target="tpu_custom_call" | custom-call | tf_op jit(solution)/shard_map/pallas_call | solution.py:551
  124.8 2.1 %shard_map.119 = bf16[512,4096]{1,0:T(8,128)(2,1)} custom-call(bf16[16,512,256]{2,1,0:T(8,128)(2,1)S(1)} %shard_map.118.blocks), custom_call_target="tpu_custom_call" | custom-call | tf_op jit(solution)/shard_map/pallas_call | solution.py:603
